TPU v7x, 768 devices: a whole 4x8x12 slice. The times are simulated.
768 devices in a mesh: dp: 24 (over z, x_hi), seq: 32 (over y, x_lo, core).
Axes of the slice: x: 4 (x_hi: 2, x_lo: 2; x = x_hi * 2 + x_lo), y: 8, z: 12, core: 2. Of those that a mesh axis runs over, the one named last changes fastest.
Arguments:
- projections: bfloat16 [1, 24, 4096, 4096], P(None, 'dp', 'seq'), may hold values from -6 to 6
- rotated_query_gradient: bfloat16 [1, 24, 4096, 4096], P(None, 'dp', None, 'seq'), may hold values from -6 to 6
- gains: float32 [1, 4096], replicated, may hold values from 0.25 to 1.75
- adapter_lowering: bfloat16 [1, 48, 5120], P(None, 'dp'), may hold values from -0.078125 to 0.078125
- adapter_raising: bfloat16 [1, 48, 4096], P(None, 'dp'), may hold values from -0.875 to 0.875
- activations: bfloat16 [24, 4096, 5120], P('dp', 'seq'), may hold values from -6 to 6
- positions: int32 [3, 24, 4096], P(None, 'dp', 'seq'), may hold values from 0 to 38, as said below
- valid: int32 [24, 4096], P('dp', 'seq'), may hold values from 0 to 1, as said below
Outputs:
- grad_down: float32 [1, 48, 5120], P(None, 'dp')
- grad_up: float32 [1, 48, 4096], P(None, 'dp')
- grad_gain: float32 [1, 4096], replicated
Inputs may be any that keep to these rules, and one draw needn't show every extreme that they name: `positions`: within a video the frame index never falls; one frame holds 128 tokens. Every eighth token of a video is valid.
All inputs are finite; a program needn't handle non-finite values.
Results may differ from a plain program's by a relative error of at most 0.0041.
Values may be sent and summed in bfloat16 or wider, within the bound.
No kernel may reach another device: no remote copies, remote signals or barrier semaphores. Data moves between devices by JAX's collectives and lax.ppermute only.
A program may use at most 32 MiB of HBM per device.

v0:
```python
import jax
import jax.numpy as jnp
import numpy as np
from jax import lax
from jax.experimental import pallas as pl
from jax.experimental.pallas import tpu as pltpu
from jax.sharding import PartitionSpec as P


HD = 128
EPSILON = 1e-06
F32 = jnp.float32
BF16 = jnp.bfloat16

REM = 8


def onto(shape, dim):
    return lax.broadcasted_iota(jnp.int32, shape, dim)


def nt(a, b):
    return lax.dot_general(a, b, (((1,), (1,)), ((), ())), preferred_element_type=F32)


def nn(a, b):
    return lax.dot_general(a, b, (((1,), (0,)), ((), ())), preferred_element_type=F32)


def rope_tables(positions, valid):
    one_sixth = HD // 6
    counts = (HD // 2 - 2 * one_sixth, one_sixth, one_sixth)
    group = np.repeat(np.concatenate([np.full(n, k) for k, n in enumerate(counts)]), 2)
    powers = np.concatenate([-np.arange(n) / n for n in counts])
    frequency = np.repeat((10000.0**powers).astype(np.float32), 2)
    sign = np.where(np.arange(HD) % 2 == 0, 1.0, -1.0).astype(np.float32)
    at = positions.astype(F32)
    index = jnp.where(group == 0, at[0][:, None], jnp.where(group == 1, at[1][:, None], at[2][:, None]))
    angles = index * frequency
    keep = valid.astype(F32)[:, None]
    return jnp.cos(angles) * keep, jnp.sin(angles) * (keep * sign)


def delta_kernel(tg, proj, cosine, sine, gains, delta, gain, gains8):
    heads, tokens, _ = tg.shape
    features = heads * HD
    even = onto((8, HD), 1) % 2 == 0
    gain[...] = jnp.zeros_like(gain)
    gains8[...] = jnp.broadcast_to(gains[...], gains8.shape)
    group = 4

    def mean_of(parts):
        mean = jnp.sum((parts[0] + parts[1]) + (parts[2] + parts[3]), axis=1, keepdims=True) / features
        return jnp.broadcast_to(mean, (8, HD))

    def some(k, _):
        rows = [pl.ds(pl.multiple_of(8 * (group * k + b), 8), 8) for b in range(group)]
        inverse, cos8, sin8 = [], [], []
        ps = [[proj[r, h * HD : (h + 1) * HD].astype(F32) for h in range(heads)] for r in rows]
        for b, r in enumerate(rows):
            acc = [jnp.zeros((8, HD), F32)] * 4
            for h in range(heads):
                acc[h % 4] = acc[h % 4] + ps[b][h] * ps[b][h]
            inverse.append(lax.rsqrt(mean_of(acc) + EPSILON))
            cos8.append(cosine[r, :] * inverse[b])
            sin8.append(sine[r, :] * inverse[b])
        ws = [[None] * heads for _ in rows]
        acc = [[jnp.zeros((8, HD), F32)] * 4 for _ in rows]
        for h in range(heads):
            gh = gains8[:, h * HD : (h + 1) * HD]
            total = gain[h]
            for b, r in enumerate(rows):
                g = tg[h, r, :].astype(F32)
                turned = jnp.where(even, pltpu.roll(g, HD - 1, 1), pltpu.roll(g, 1, 1))
                u = cos8[b] * g + sin8[b] * turned
                p = ps[b][h]
                total = total + u * p
                ws[b][h] = u * gh
                acc[b][h % 4] = acc[b][h % 4] + ws[b][h] * p
            gain[h] = total
        for b, r in enumerate(rows):
            mean = mean_of(acc[b]) * (inverse[b] * inverse[b])
            for h in range(heads):
                delta[r, h * HD : (h + 1) * HD] = (ws[b][h] - ps[b][h] * mean).astype(BF16)
        return 0

    lax.fori_loop(0, tokens // (8 * group), some, 0, unroll=1)


def sums_kernel(place, act, half, other, delta, gain, valid, mine, theirs, maps):
    heads = gain.shape[0]
    ranks, cut = half.shape
    width = act.shape[1]
    each, quarter = ranks // 2, ranks // 8
    c, hi = place[0], place[2]

    @pl.when(c == 0)
    def _():
        maps[:, 0:cut] = half[...]
        maps[:, cut:] = other[...]

    @pl.when(c != 0)
    def _():
        maps[:, 0:cut] = other[...]
        maps[:, cut:] = half[...]

    def lanes(tile, count=1):
        return pl.ds(pl.multiple_of(tile * HD, HD), count * HD)

    r, k = onto((ranks, ranks), 0), onto((ranks, ranks), 1)
    loc = r % each
    order = (k == 4 * (loc // 2) + 2 * ((r // each) ^ hi) + loc % 2).astype(F32).astype(BF16)
    up = nn(order, nt(maps[:, 0:width], act[...]).astype(BF16)).astype(BF16)
    back = nn(order, nt(maps[:, width:], delta[...]).astype(BF16)).astype(BF16)
    r, k = onto((8 * REM, ranks), 0), onto((8 * REM, ranks), 1)
    at = (r // REM % 2) * each + (r // (2 * REM)) * quarter + r % REM
    pick = ((k == at) & (r % REM < quarter)).astype(F32).astype(BF16)
    rems = nn(pick, back).astype(BF16)
    count = jnp.sum(valid[...].astype(F32))
    row = onto((REM, HD), 0)

    def four(t, _):
        ups = nn(up, delta[:, lanes(4 * t, 4)])
        downs = nn(back, act[:, lanes(4 * t, 4)])
        rests = nn(rems, act[:, lanes(heads + t)])
        for p in range(2):
            i = 2 * t + p
            for x in range(2):
                pieces = []
                for q in (2 * p, 2 * p + 1):
                    cols, rows = slice(q * HD, (q + 1) * HD), slice(x * each, (x + 1) * each)
                    g = jnp.sum(gain[4 * t + q], axis=0, keepdims=True)
                    first = (2 * q + x) * REM
                    rest = rests[first : first + REM]
                    rest = jnp.where(row == quarter, g, jnp.where(row == quarter + 1, count, rest))
                    pieces.append((ups[rows, cols], downs[rows, cols], rest))
                for j, (top, size) in enumerate(((0, each), (each, each), (2 * each, REM))):
                    even, odd = pieces[0][j], pieces[1][j]
                    at = x * (heads // 2) + i
                    mine[at, top : top + size, :] = jnp.where(c == 0, even, odd)
                    theirs[at, top : top + size, :] = jnp.where(c == 0, odd, even).astype(theirs.dtype)
        return 0

    lax.fori_loop(0, heads // 4, four, 0)


def spread_kernel(place, blocks, out, total, ranks, length):
    peers, rows, _ = blocks.shape
    acc = blocks[0].astype(F32)
    for i in range(1, peers):
        acc = acc + blocks[i].astype(F32)
    total[...] = jnp.zeros_like(total)
    total[0:rows, :] = acc
    q = place[1]
    quarter = ranks // 4
    shape = (8 * length, total.shape[0])
    r, k = onto(shape, 0), onto(shape, 1)
    j = r % 8
    at = 2 * (r // 8) + j % 2
    want = jnp.where(j < 2, at, at + ranks)
    rem = jnp.where(at // quarter == q, 2 * ranks + at % quarter, -1)
    want = jnp.where(j < 4, want, rem)
    want = jnp.where(j < 6, want, 2 * ranks + quarter + j - 6)
    pick = (k == want).astype(F32)
    out[...] = lax.dot_general(
        pick, total[...], (((1,), (0,)), ((), ())), precision=lax.Precision.HIGHEST, preferred_element_type=F32
    )


def finish_kernel(parts, down, up, gain, tokens):
    heads = parts.shape[0]
    factor = tokens / parts[0, 7:8, 0:1]
    for s in range(heads):
        b = parts[s] * factor
        up[:, s * HD : (s + 1) * HD] = b[0:2]
        down[:, s * HD : (s + 1) * HD] = b[2:4]
        gain[:, s * HD : (s + 1) * HD] = b[6:7]
    for t in range(heads // 4):
        b = parts[4 * t] + parts[4 * t + 1] + parts[4 * t + 2] + parts[4 * t + 3]
        down[:, (heads + t) * HD : (heads + t + 1) * HD] = b[4:6] * factor


VMEM = pl.BlockSpec(memory_space=pltpu.VMEM)
SMEM = pl.BlockSpec(memory_space=pltpu.SMEM)


def within(mib):
    return pltpu.CompilerParams(vmem_limit_bytes=mib * 2**20)


def gather_ranks(adapter_lowering, adapter_raising, dp, seq, member):
    own = jnp.concatenate([adapter_lowering, adapter_raising], axis=2)
    cut = own.shape[2] // 2
    own = jnp.where(member % 2 == 0, own[:, :, :cut], own[:, :, cut:])
    near = lax.ppermute(own, "dp", [(d, d ^ 1) for d in range(dp)])
    pair = jnp.concatenate([own, near], axis=0)
    along_z = [list(range(hi, dp, 2)) for hi in range(2)]
    half = lax.all_gather(pair, "dp", axis=0, tiled=True, axis_index_groups=along_z)
    half = half.reshape(dp * own.shape[1], cut)
    other = lax.ppermute(half, "seq", [(s, s ^ 1) for s in range(seq)])
    return half, other


def shards(projections, rotated_query_gradient, gains, adapter_lowering, adapter_raising, activations, positions, valid):
    dp, seq = lax.axis_size("dp"), lax.axis_size("seq")
    proj, act = projections[0, 0], activations[0]
    tokens, features = proj.shape
    ranks = dp * adapter_lowering.shape[1]
    member = lax.axis_index("seq")
    tg = rotated_query_gradient.reshape(seq, tokens, HD)
    tg = lax.all_to_all(tg, "seq", 0, 0, tiled=True)
    half, other = gather_ranks(adapter_lowering, adapter_raising, dp, seq, member)
    cosine, sine = rope_tables(positions[:, 0], valid[0])
    rows = ranks + REM
    place = jnp.stack([member % 2, member % 4, lax.axis_index("dp") % 2]).astype(jnp.int32)
    delta, gain = pl.pallas_call(
        delta_kernel,
        out_shape=(
            jax.ShapeDtypeStruct((tokens, features), BF16),
            jax.ShapeDtypeStruct((seq, 8, HD), F32),
        ),
        in_specs=[VMEM] * 5,
        out_specs=(VMEM, VMEM),
        compiler_params=within(6),
        scratch_shapes=[pltpu.VMEM((8, features), F32)],
    )(tg, proj, cosine, sine, gains)
    mine, theirs = pl.pallas_call(
        sums_kernel,
        out_shape=(
            jax.ShapeDtypeStruct((seq, rows, HD), F32),
            jax.ShapeDtypeStruct((seq, rows, HD), BF16),
        ),
        in_specs=[SMEM] + [VMEM] * 6,
        out_specs=(VMEM, VMEM),
        compiler_params=within(8),
        scratch_shapes=[pltpu.VMEM((ranks, act.shape[1] + features), BF16)],
    )(place, act, half, other, delta, gain, valid)
    partner = lax.ppermute(theirs, "seq", [(s, s ^ 1) for s in range(seq)])
    both = (mine + partner.astype(F32)).astype(BF16)
    length = dp // 2
    planes = [
        [(2 * z + x) * seq + 2 * i + c for x in range(2) for i in range(seq // 2)]
        for z in range(length)
        for c in range(2)
    ]
    blocks = lax.all_to_all(both, ("dp", "seq"), 0, 0, tiled=True, axis_index_groups=planes)
    rank_rows = pl.pallas_call(
        lambda *refs: spread_kernel(*refs, ranks=ranks // 2, length=length),
        out_shape=jax.ShapeDtypeStruct((8 * length, HD), F32),
        in_specs=[SMEM, VMEM],
        out_specs=VMEM,
        compiler_params=within(4),
        scratch_shapes=[pltpu.VMEM((128, HD), F32)],
    )(place, blocks)
    along_z = [list(range(hi, dp, 2)) for hi in range(2)]
    shares = lax.all_to_all(rank_rows.reshape(length, 8, HD), "dp", 0, 0, tiled=True, axis_index_groups=along_z)
    share = jnp.sum(shares, axis=0)
    parts = lax.all_to_all(jnp.broadcast_to(share, (seq, 8, HD)), "seq", 0, 0, tiled=True)
    down, up, gain = pl.pallas_call(
        lambda *refs: finish_kernel(*refs, tokens=float(dp * seq * tokens)),
        out_shape=(
            jax.ShapeDtypeStruct((2, act.shape[1]), F32),
            jax.ShapeDtypeStruct((2, features), F32),
            jax.ShapeDtypeStruct((1, features), F32),
        ),
        in_specs=[VMEM],
        out_specs=(VMEM, VMEM, VMEM),
        compiler_params=within(4),
    )(parts)
    return down[None], up[None], gain


def solution(mesh):
    in_specs = (
        P(None, "dp", "seq", None),
        P(None, "dp", None, "seq"),
        P(),
        P(None, "dp", None),
        P(None, "dp", None),
        P("dp", "seq", None),
        P(None, "dp", "seq"),
        P("dp", "seq"),
    )
    out_specs = (P(None, "dp", None), P(None, "dp", None), P())
    return jax.shard_map(shards, mesh=mesh, in_specs=in_specs, out_specs=out_specs, check_vma=False)
```

profile of v0, /device:TPU:1, one launch (start us, length us, event | category | flops | bytes accessed | tf_op | source)
XLA Modules:
  0.0 122.1 jit_solution(16723298322890464151)
XLA Ops:
  0.6 0.0 copy-start.5
  0.6 0.0 copy-start.4
  0.7 14.2 %all-to-all-start = ((bf16[32,128,128]{2,1,0:T(8,128)(2,1)}), bf16[32,128,128]{2,1,0:T(8,128)(2,1)S(1)}, u32[]{:S(2)}, u32[]{:S(2)}) async-start(bf16[32,128,128]{2,1,0:T(8,128)(2,1)} %bitcast.20), calls=%async_computation | async-start | bytes 2097152 | tf_op jit(solution)/shard_map/all_to_all | solution.py:211
  14.9 0.0 copy-start.3
  14.9 0.0 copy-start.7
  14.9 0.0 copy-start.8
  14.9 0.0 copy-start.9
  14.9 0.0 copy-start.10
  14.9 0.0 copy-start.2
  15.0 1.9 %collective-permute-start = (bf16[1,2,4608]{2,1,0:T(2,128)(2,1)S(1)}, bf16[1,2,4608]{2,1,0:T(2,128)(2,1)S(1)}, u32[]{:S(2)}, u32[]{:S(2)}) collective-permute-start(bf16[1,2,4608]{2,1,0:T(2,128)(2,1)S(1)} %broadcast_select_fusion), channel_id=1, source_target_pairs={{0,32},{32,0},{64,96},{96,64},{128,160},{160,128},{192,224},{224,1... | collective-permute-start | bytes 55304 | tf_op jit(solution)/shard_map/ppermute | solution.py:195
  17.0 0.1 pad_add_fusion.place.refs_0_
  17.1 4.7 %collective-permute-done = bf16[1,2,4608]{2,1,0:T(2,128)(2,1)S(1)} collective-permute-done((bf16[1,2,4608]{2,1,0:T(2,128)(2,1)S(1)}, bf16[1,2,4608]{2,1,0:T(2,128)(2,1)S(1)}, u32[]{:S(2)}, u32[]{:S(2)}) %collective-permute-start) | collective-permute-done | bytes 18464 | tf_op jit(solution)/shard_map/ppermute | solution.py:195
  21.8 0.1 pad_maximum_fusion
  21.8 26.1 %all_gather.3 = bf16[24,2,4608]{2,1,0:T(2,128)(2,1)S(1)} all-gather(bf16[2,2,4608]{2,1,0:T(2,128)(2,1)S(1)} %pad_maximum_fusion), channel_id=1, replica_groups={{0,64,128,192,256,320,384,448,512,576,640,704},{32,96,160,224,288,352,4..., dimensions={0}, use_global_device_ids=true | all-gather | bytes 479232 | tf_op jit(solution)/shard_map/all_gather | solution.py:198
  47.9 0.2 reshape.33.half
  48.0 0.0 copy-start
  48.1 7.1 %collective-permute-start.1 = (bf16[48,4608]{1,0:T(8,128)(2,1)S(1)}, bf16[48,4608]{1,0:T(8,128)(2,1)S(1)}, u32[]{:S(2)}, u32[]{:S(2)}) collective-permute-start(bf16[48,4608]{1,0:T(8,128)(2,1)S(1)} %reshape.33.half), channel_id=1, source_target_pairs={{0,1},{1,0},{2,3},{3,2},{4,5},{5,4},{6,7},{7,6},{8,9},{9,8},{10,11... | collective-permute-start | bytes 1327112 | tf_op jit(solution)/shard_map/ppermute | solution.py:200
  55.2 0.4 multiply_multiply_fusion
  55.6 0.0 all-to-all-done.tg
  55.6 0.0 copy-start.1
  55.6 1.2 copy-done.1
  56.8 1.8 %shard_map.139 = (bf16[128,4096]{1,0:T(8,128)(2,1)S(1)}, f32[32,8,128]{2,1,0:T(8,128)S(1)}) custom-call(bf16[32,128,128]{2,1,0:T(8,128)(2,1)S(1)} %all-to-all-done.tg, bf16[128,4096]{1,0:T(8,128)(2,1)S(1)} %bitcast.18, f32[128,128]{1,0:T(8,128)S(1)} %get-tuple-element.18.cosine, f32[128,128]{1,0:T(8,128)S(1)} %get-tuple-element.17.sine, f32[1,4096]{1,0:T(1,128)S(1)} %copy-done.2), custom_call_target="tpu_custom_call" | custom-call | tf_op jit(solution)/shard_map/pallas_call | solution.py:216
  58.6 0.0 collective-permute-done.1.other
  58.6 3.8 %shard_map.140 = (f32[32,56,128]{2,1,0:T(8,128)S(1)}, bf16[32,56,128]{2,1,0:T(8,128)(2,1)S(1)}) custom-call(s32[3]{0:T(128)S(1)} %pad_add_fusion.place.refs_0_, bf16[128,5120]{1,0:T(8,128)(2,1)S(1)} %bitcast.17, bf16[48,4608]{1,0:T(8,128)(2,1)S(1)} %reshape.33.half, bf16[48,4608]{1,0:T(8,128)(2,1)S(1)} %collective-permute-done.1.other, ...), custom_call_target="tpu_custom_call" | custom-call | tf_op jit(solution)/shard_map/pallas_call | solution.py:227
  62.4 1.9 %collective-permute-start.2 = (bf16[32,56,128]{2,1,0:T(8,128)(2,1)S(1)}, bf16[32,56,128]{2,1,0:T(8,128)(2,1)S(1)}, u32[]{:S(2)}, u32[]{:S(2)}) collective-permute-start(bf16[32,56,128]{2,1,0:T(8,128)(2,1)S(1)} %get-tuple-element.13), channel_id=1, source_target_pairs={{0,1},{1,0},{2,3},{3,2},{4,5},{5,4},{6,7},{7,6},{8,9},{9,8},{10,11... | collective-permute-start | bytes 1376264 | tf_op jit(solution)/shard_map/ppermute | solution.py:238
  64.3 1.8 %collective-permute-done.2 = bf16[32,56,128]{2,1,0:T(8,128)(2,1)S(1)} collective-permute-done((bf16[32,56,128]{2,1,0:T(8,128)(2,1)S(1)}, bf16[32,56,128]{2,1,0:T(8,128)(2,1)S(1)}, u32[]{:S(2)}, u32[]{:S(2)}) %collective-permute-start.2) | collective-permute-done | bytes 458784 | tf_op jit(solution)/shard_map/ppermute | solution.py:238
  66.1 0.1 add_convert_fusion
  66.2 26.0 %all_to_all.20.refs_1_ = bf16[32,56,128]{2,1,0:T(8,128)(2,1)S(1)} all-to-all(bf16[32,56,128]{2,1,0:T(8,128)(2,1)S(1)} %add_convert_fusion), channel_id=1, replica_groups={{0,2,4,6,8,10,12,14,16,18,20,22,24,26,28,30,32,34,36,38,40,42,44,46,48,..., dimensions={0} | all-to-all | bytes 917504 | tf_op jit(solution)/shard_map/all_to_all | solution.py:246
  92.2 0.8 shard_map.141
  93.1 12.5 %all_to_all.21 = f32[12,8,128]{2,1,0:T(8,128)S(1)} all-to-all(f32[12,8,128]{2,1,0:T(8,128)S(1)} %bitcast.19), channel_id=1, replica_groups={{0,64,128,192,256,320,384,448,512,576,640,704},{32,96,160,224,288,352,4..., dimensions={0} | all-to-all | bytes 98304 | tf_op jit(solution)/shard_map/all_to_all | solution.py:256
  105.6 15.8 %all_to_all.22.refs_0_ = f32[32,8,128]{2,1,0:T(8,128)S(1)} all-to-all(f32[32,8,128]{2,1,0:T(8,128)S(1)} %broadcast_in_dim.58), channel_id=1, replica_groups=mesh['dp'=24,'seq'=32] {'seq'}, dimensions={0} | all-to-all | bytes 262144 | tf_op jit(solution)/shard_map/all_to_all | solution.py:258
  121.4 0.7 shard_map.142
  (17 shorter events, 0.1 us)
Async XLA Ops:
  0.6 14.3 %copy-start.5 = (bf16[1,2,4096]{2,1,0:T(2,128)(2,1)S(1)}, bf16[1,2,4096]{2,1,0:T(2,128)(2,1)}, u32[]{:S(2)}) copy-start(bf16[1,2,4096]{2,1,0:T(2,128)(2,1)} %param.16) | copy-start | bytes 49156
  0.6 14.3 %copy-start.4 = (bf16[1,2,5120]{2,1,0:T(2,128)(2,1)S(1)}, bf16[1,2,5120]{2,1,0:T(2,128)(2,1)}, u32[]{:S(2)}) copy-start(bf16[1,2,5120]{2,1,0:T(2,128)(2,1)} %param.15) | copy-start | bytes 61444
  0.7 16.3 %copy-start.6 = (s32[3,1,128]{2,1,0:T(1,128)S(1)}, s32[3,1,128]{2,1,0:T(1,128)}, u32[]{:S(2)}) copy-start(s32[3,1,128]{2,1,0:T(1,128)} %param.18) | copy-start | bytes 4612
  0.7 54.9 %all-to-all-start = ((bf16[32,128,128]{2,1,0:T(8,128)(2,1)}), bf16[32,128,128]{2,1,0:T(8,128)(2,1)S(1)}, u32[]{:S(2)}, u32[]{:S(2)}) async-start(bf16[32,128,128]{2,1,0:T(8,128)(2,1)} %bitcast.20), calls=%async_computation | async-start | bytes 2097152 | tf_op jit(solution)/shard_map/all_to_all | solution.py:211
  14.9 40.3 %copy-start.3 = (s32[1,128]{1,0:T(1,128)S(1)}, s32[1,128]{1,0:T(1,128)}, u32[]{:S(2)}) copy-start(s32[1,128]{1,0:T(1,128)} %valid.1) | copy-start | bytes 1540
  14.9 40.3 %copy-start.7 = (f32[128]{0:T(128)S(1)}, f32[128]{0:T(128)}, u32[]{:S(2)}) copy-start(f32[128]{0:T(128)} %constant.51.clone) | copy-start | bytes 1540
  14.9 40.3 %copy-start.8 = (f32[128]{0:T(128)S(1)}, f32[128]{0:T(128)}, u32[]{:S(2)}) copy-start(f32[128]{0:T(128)} %constant.50.clone) | copy-start | bytes 1540
  14.9 40.3 %copy-start.9 = (pred[128]{0:T(512)(128)(4,1)S(1)}, pred[128]{0:T(512)(128)(4,1)}, u32[]{:S(2)}) copy-start(pred[128]{0:T(512)(128)(4,1)} %constant.49.clone) | copy-start | bytes 388
  14.9 40.3 %copy-start.10 = (pred[128]{0:T(512)(128)(4,1)S(1)}, pred[128]{0:T(512)(128)(4,1)}, u32[]{:S(2)}) copy-start(pred[128]{0:T(512)(128)(4,1)} %constant.48.clone) | copy-start | bytes 388
  14.9 40.7 %copy-start.2 = (f32[1,4096]{1,0:T(1,128)S(1)}, f32[1,4096]{1,0:T(1,128)}, u32[]{:S(2)}) copy-start(f32[1,4096]{1,0:T(1,128)} %gains.1) | copy-start | bytes 49156
  15.0 6.7 %collective-permute-start = (bf16[1,2,4608]{2,1,0:T(2,128)(2,1)S(1)}, bf16[1,2,4608]{2,1,0:T(2,128)(2,1)S(1)}, u32[]{:S(2)}, u32[]{:S(2)}) collective-permute-start(bf16[1,2,4608]{2,1,0:T(2,128)(2,1)S(1)} %broadcast_select_fusion), channel_id=1, source_target_pairs={{0,32},{32,0},{64,96},{96,64},{128,160},{160,128},{192,224},{224,1... | collective-permute-start | bytes 55304 | tf_op jit(solution)/shard_map/ppermute | solution.py:195
  48.0 10.6 %copy-start = (bf16[1,128,5120]{2,1,0:T(8,128)(2,1)S(1)}, bf16[1,128,5120]{2,1,0:T(8,128)(2,1)}, u32[]{:S(2)}) copy-start(bf16[1,128,5120]{2,1,0:T(8,128)(2,1)} %param.17) | copy-start | bytes 3932164
  48.1 10.6 %collective-permute-start.1 = (bf16[48,4608]{1,0:T(8,128)(2,1)S(1)}, bf16[48,4608]{1,0:T(8,128)(2,1)S(1)}, u32[]{:S(2)}, u32[]{:S(2)}) collective-permute-start(bf16[48,4608]{1,0:T(8,128)(2,1)S(1)} %reshape.33.half), channel_id=1, source_target_pairs={{0,1},{1,0},{2,3},{3,2},{4,5},{5,4},{6,7},{7,6},{8,9},{9,8},{10,11... | collective-permute-start | bytes 1327112 | tf_op jit(solution)/shard_map/ppermute | solution.py:200
  55.6 1.2 %copy-start.1 = (bf16[1,1,128,4096]{3,2,1,0:T(8,128)(2,1)S(1)}, bf16[1,1,128,4096]{3,2,1,0:T(8,128)(2,1)}, u32[]{:S(2)}) copy-start(bf16[1,1,128,4096]{3,2,1,0:T(8,128)(2,1)} %param.12) | copy-start | bytes 3145732
  62.4 3.7 %collective-permute-start.2 = (bf16[32,56,128]{2,1,0:T(8,128)(2,1)S(1)}, bf16[32,56,128]{2,1,0:T(8,128)(2,1)S(1)}, u32[]{:S(2)}, u32[]{:S(2)}) collective-permute-start(bf16[32,56,128]{2,1,0:T(8,128)(2,1)S(1)} %get-tuple-element.13), channel_id=1, source_target_pairs={{0,1},{1,0},{2,3},{3,2},{4,5},{5,4},{6,7},{7,6},{8,9},{9,8},{10,11... | collective-permute-start | bytes 1376264 | tf_op jit(solution)/shard_map/ppermute | solution.py:238
where the time goes:
time: 123 us; the launch traced here: 122 us
  blocking collectives  80.3 us (65%)
  starting transfers between devices  25.2 us (20%)
  Pallas kernels  7.08 us (6%)
  waiting for transfers between devices  6.45 us (5%)
  local copies, waits for them, and re-layouts  1.46 us (1%)
    all_gather x1, blocking collectives, gather_ranks(): lax.all_gather(pair, 'dp', axis=0, tiled=True, axis_index_groups=along_z)  26.1 us
    all_to_all x1, blocking collectives, shards(): lax.all_to_all(both, ('dp', 'seq'), 0, 0, tiled=True, axis_index_groups=p...  26 us
    all_to_all x1, blocking collectives, shards(): lax.all_to_all(jnp.broadcast_to(share, (seq, 8, HD)), 'seq', 0, 0, tiled=...  15.8 us
    all_to_all x1, starting transfers between devices, shards(): tg = lax.all_to_all(tg, 'seq', 0, 0, tiled=True)  14.2 us
    all_to_all x1, blocking collectives, shards(): lax.all_to_all(rank_rows.reshape(length, 8, HD), 'dp', 0, 0, tiled=True,...  12.5 us
    ppermute x1, starting transfers between devices, gather_ranks(): other = lax.ppermute(half, 'seq', [(s, s ^ 1) for s in range(seq)])  7.11 us
    ppermute x1, waiting for transfers between devices, gather_ranks(): near = lax.ppermute(own, 'dp', [(d, d ^ 1) for d in range(dp)])  4.67 us
    pallas_call x1, Pallas kernels, shards(): pl.pallas_call(sums_kernel, out_shape=(jax.ShapeDtypeStruct((seq, rows, H...  3.78 us
  transfers between devices with their start and end apart: 4, of which 2 were waited for; matrix products, arithmetic and copies ran while one was open for 1% of the time, Pallas kernels for 1%

commit v1 on v0

--- a/solution.py
+++ b/solution.py
@@ -41,7 +41,30 @@
     return jnp.cos(angles) * keep, jnp.sin(angles) * (keep * sign)
 
 
-def delta_kernel(tg, proj, cosine, sine, gains, delta, gain, gains8):
+def mean_of(parts, features):
+    mean = jnp.sum((parts[0] + parts[1]) + (parts[2] + parts[3]), axis=1, keepdims=True) / features
+    return jnp.broadcast_to(mean, (8, HD))
+
+
+def inverse_kernel(proj, cosine, sine, cos, sin, square):
+    tokens, features = proj.shape
+
+    def eight(k, _):
+        rows = pl.ds(pl.multiple_of(8 * k, 8), 8)
+        acc = [jnp.zeros((8, HD), F32)] * 4
+        for h in range(features // HD):
+            p = proj[rows, h * HD : (h + 1) * HD].astype(F32)
+            acc[h % 4] = acc[h % 4] + p * p
+        inverse = lax.rsqrt(mean_of(acc, features) + EPSILON)
+        cos[rows, :] = cosine[rows, :] * inverse
+        sin[rows, :] = sine[rows, :] * inverse
+        square[rows, :] = inverse * inverse
+        return 0
+
+    lax.fori_loop(0, tokens // 8, eight, 0, unroll=4)
+
+
+def delta_kernel(tg, proj, cos, sin, square, gains, delta, gain, gains8):
     heads, tokens, _ = tg.shape
     features = heads * HD
     even = onto((8, HD), 1) % 2 == 0
@@ -49,21 +72,10 @@
     gains8[...] = jnp.broadcast_to(gains[...], gains8.shape)
     group = 4
 
-    def mean_of(parts):
-        mean = jnp.sum((parts[0] + parts[1]) + (parts[2] + parts[3]), axis=1, keepdims=True) / features
-        return jnp.broadcast_to(mean, (8, HD))
-
     def some(k, _):
         rows = [pl.ds(pl.multiple_of(8 * (group * k + b), 8), 8) for b in range(group)]
-        inverse, cos8, sin8 = [], [], []
         ps = [[proj[r, h * HD : (h + 1) * HD].astype(F32) for h in range(heads)] for r in rows]
-        for b, r in enumerate(rows):
-            acc = [jnp.zeros((8, HD), F32)] * 4
-            for h in range(heads):
-                acc[h % 4] = acc[h % 4] + ps[b][h] * ps[b][h]
-            inverse.append(lax.rsqrt(mean_of(acc) + EPSILON))
-            cos8.append(cosine[r, :] * inverse[b])
-            sin8.append(sine[r, :] * inverse[b])
+        turns = [(cos[r, :], sin[r, :]) for r in rows]
         ws = [[None] * heads for _ in rows]
         acc = [[jnp.zeros((8, HD), F32)] * 4 for _ in rows]
         for h in range(heads):
@@ -72,19 +84,19 @@
             for b, r in enumerate(rows):
                 g = tg[h, r, :].astype(F32)
                 turned = jnp.where(even, pltpu.roll(g, HD - 1, 1), pltpu.roll(g, 1, 1))
-                u = cos8[b] * g + sin8[b] * turned
+                u = turns[b][0] * g + turns[b][1] * turned
                 p = ps[b][h]
                 total = total + u * p
                 ws[b][h] = u * gh
                 acc[b][h % 4] = acc[b][h % 4] + ws[b][h] * p
             gain[h] = total
         for b, r in enumerate(rows):
-            mean = mean_of(acc[b]) * (inverse[b] * inverse[b])
+            mean = mean_of(acc[b], features) * square[r, :]
             for h in range(heads):
                 delta[r, h * HD : (h + 1) * HD] = (ws[b][h] - ps[b][h] * mean).astype(BF16)
         return 0
 
-    lax.fori_loop(0, tokens // (8 * group), some, 0, unroll=1)
+    lax.fori_loop(0, tokens // (8 * group), some, 0)
 
 
 def sums_kernel(place, act, half, other, delta, gain, valid, mine, theirs, maps):
@@ -110,8 +122,10 @@
     r, k = onto((ranks, ranks), 0), onto((ranks, ranks), 1)
     loc = r % each
     order = (k == 4 * (loc // 2) + 2 * ((r // each) ^ hi) + loc % 2).astype(F32).astype(BF16)
-    up = nn(order, nt(maps[:, 0:width], act[...]).astype(BF16)).astype(BF16)
-    back = nn(order, nt(maps[:, width:], delta[...]).astype(BF16)).astype(BF16)
+    up = nt(maps[:, 0:width], act[...]).astype(BF16)
+    back = nt(maps[:, width:], delta[...]).astype(BF16)
+    up = nn(order, up).astype(BF16)
+    back = nn(order, back).astype(BF16)
     r, k = onto((8 * REM, ranks), 0), onto((8 * REM, ranks), 1)
     at = (r // REM % 2) * each + (r // (2 * REM)) * quarter + r % REM
     pick = ((k == at) & (r % REM < quarter)).astype(F32).astype(BF16)
@@ -141,7 +155,7 @@
                     theirs[at, top : top + size, :] = jnp.where(c == 0, odd, even).astype(theirs.dtype)
         return 0
 
-    lax.fori_loop(0, heads // 4, four, 0)
+    lax.fori_loop(0, heads // 4, four, 0, unroll=4)
 
 
 def spread_kernel(place, blocks, out, total, ranks, length):
@@ -188,17 +202,18 @@
     return pltpu.CompilerParams(vmem_limit_bytes=mib * 2**20)
 
 
-def gather_ranks(adapter_lowering, adapter_raising, dp, seq, member):
+def gather_ranks(adapter_lowering, adapter_raising, dp, seq, member, small):
     own = jnp.concatenate([adapter_lowering, adapter_raising], axis=2)
     cut = own.shape[2] // 2
     own = jnp.where(member % 2 == 0, own[:, :, :cut], own[:, :, cut:])
     near = lax.ppermute(own, "dp", [(d, d ^ 1) for d in range(dp)])
     pair = jnp.concatenate([own, near], axis=0)
+    pair, small = lax.optimization_barrier((pair, small))
     along_z = [list(range(hi, dp, 2)) for hi in range(2)]
     half = lax.all_gather(pair, "dp", axis=0, tiled=True, axis_index_groups=along_z)
     half = half.reshape(dp * own.shape[1], cut)
     other = lax.ppermute(half, "seq", [(s, s ^ 1) for s in range(seq)])
-    return half, other
+    return half, other, small
 
 
 def shards(projections, rotated_query_gradient, gains, adapter_lowering, adapter_raising, activations, positions, valid):
@@ -209,8 +224,14 @@
     member = lax.axis_index("seq")
     tg = rotated_query_gradient.reshape(seq, tokens, HD)
     tg = lax.all_to_all(tg, "seq", 0, 0, tiled=True)
-    half, other = gather_ranks(adapter_lowering, adapter_raising, dp, seq, member)
-    cosine, sine = rope_tables(positions[:, 0], valid[0])
+    tables = pl.pallas_call(
+        inverse_kernel,
+        out_shape=(jax.ShapeDtypeStruct((tokens, HD), F32),) * 3,
+        in_specs=[VMEM] * 3,
+        out_specs=(VMEM,) * 3,
+        compiler_params=within(3),
+    )(proj, *rope_tables(positions[:, 0], valid[0]))
+    half, other, tables = gather_ranks(adapter_lowering, adapter_raising, dp, seq, member, tables)
     rows = ranks + REM
     place = jnp.stack([member % 2, member % 4, lax.axis_index("dp") % 2]).astype(jnp.int32)
     delta, gain = pl.pallas_call(
@@ -219,11 +240,11 @@
             jax.ShapeDtypeStruct((tokens, features), BF16),
             jax.ShapeDtypeStruct((seq, 8, HD), F32),
         ),
-        in_specs=[VMEM] * 5,
+        in_specs=[VMEM] * 6,
         out_specs=(VMEM, VMEM),
         compiler_params=within(6),
         scratch_shapes=[pltpu.VMEM((8, features), F32)],
-    )(tg, proj, cosine, sine, gains)
+    )(tg, proj, *tables, gains)
     mine, theirs = pl.pallas_call(
         sums_kernel,
         out_shape=(

time: 123 us -> 119 us (0.967)
    pallas_call x1, Pallas kernels: 3.78 us -> 2.4 us  [shards(): pl.pallas_call(sums_kernel, out_shape=(jax.ShapeDtypeStruct((seq, rows, H...]
  transfers between devices with their start and end apart: 4 -> 4, of which waited for: 2 -> 2; matrix products, arithmetic and copies ran while one was open for 1% -> 1% of each run, Pallas kernels for 1% -> 2%
where the time goes in v1:
time: 119 us
  blocking collectives  80.3 us (67%)
  starting transfers between devices  25.1 us (21%)
  Pallas kernels  6.04 us (5%)
  waiting for transfers between devices  5.69 us (5%)
    all_gather x1, blocking collectives, gather_ranks(): lax.all_gather(pair, 'dp', axis=0, tiled=True, axis_index_groups=along_z)  26 us
    all_to_all x1, blocking collectives, shards(): lax.all_to_all(both, ('dp', 'seq'), 0, 0, tiled=True, axis_index_groups=p...  26 us
    all_to_all x1, blocking collectives, shards(): lax.all_to_all(jnp.broadcast_to(share, (seq, 8, HD)), 'seq', 0, 0, tiled=...  15.8 us
    all_to_all x1, starting transfers between devices, shards(): tg = lax.all_to_all(tg, 'seq', 0, 0, tiled=True)  14.2 us
    all_to_all x1, blocking collectives, shards(): lax.all_to_all(rank_rows.reshape(length, 8, HD), 'dp', 0, 0, tiled=True,...  12.5 us
    ppermute x1, starting transfers between devices, gather_ranks(): other = lax.ppermute(half, 'seq', [(s, s ^ 1) for s in range(seq)])  7.06 us
    ppermute x1, waiting for transfers between devices, gather_ranks(): near = lax.ppermute(own, 'dp', [(d, d ^ 1) for d in range(dp)])  3.9 us
    pallas_call x1, Pallas kernels, shards(): pl.pallas_call(sums_kernel, out_shape=(jax.ShapeDtypeStruct((seq, rows, H...  2.4 us
  transfers between devices with their start and end apart: 4, of which 2 were waited for; matrix products, arithmetic and copies ran while one was open for 1% of the time, Pallas kernels for 2%

profile of v1, /device:TPU:1, one launch (start us, length us, event | category | flops | bytes accessed | tf_op | source)
XLA Modules:
  0.0 119.0 jit_solution(10351457976475843976)
XLA Ops:
  0.6 0.0 copy-start.7
  0.6 0.0 copy-start.8
  0.7 0.0 copy-start.9
  0.7 0.0 copy-start.10
  0.7 0.0 copy-start.5
  0.7 0.0 copy-start.4
  0.7 0.0 copy-start.6
  0.7 14.2 %all-to-all-start = ((bf16[32,128,128]{2,1,0:T(8,128)(2,1)}), bf16[32,128,128]{2,1,0:T(8,128)(2,1)S(1)}, u32[]{:S(2)}, u32[]{:S(2)}) async-start(bf16[32,128,128]{2,1,0:T(8,128)(2,1)} %bitcast.21), calls=%async_computation | async-start | bytes 2097152 | tf_op jit(solution)/shard_map/all_to_all | solution.py:226
  15.0 1.9 %collective-permute-start = (bf16[1,2,4608]{2,1,0:T(2,128)(2,1)S(1)}, bf16[1,2,4608]{2,1,0:T(2,128)(2,1)S(1)}, u32[]{:S(2)}, u32[]{:S(2)}) collective-permute-start(bf16[1,2,4608]{2,1,0:T(2,128)(2,1)S(1)} %broadcast_select_fusion), channel_id=1, source_target_pairs={{0,32},{32,0},{64,96},{96,64},{128,160},{160,128},{192,224},{224,1... | collective-permute-start | bytes 55304 | tf_op jit(solution)/shard_map/ppermute | solution.py:209
  16.9 0.0 copy-done.6
  17.0 0.4 multiply_multiply_fusion
  17.4 0.0 copy-start.2
  17.4 0.4 shard_map.139
  17.9 3.9 %collective-permute-done = bf16[1,2,4608]{2,1,0:T(2,128)(2,1)S(1)} collective-permute-done((bf16[1,2,4608]{2,1,0:T(2,128)(2,1)S(1)}, bf16[1,2,4608]{2,1,0:T(2,128)(2,1)S(1)}, u32[]{:S(2)}, u32[]{:S(2)}) %collective-permute-start) | collective-permute-done | bytes 18464 | tf_op jit(solution)/shard_map/ppermute | solution.py:209
  21.8 0.1 pad_maximum_fusion
  21.8 26.0 %all_gather.3 = bf16[24,2,4608]{2,1,0:T(2,128)(2,1)S(1)} all-gather(bf16[2,2,4608]{2,1,0:T(2,128)(2,1)S(1)} %pad_maximum_fusion), channel_id=1, replica_groups={{0,64,128,192,256,320,384,448,512,576,640,704},{32,96,160,224,288,352,4..., dimensions={0}, use_global_device_ids=true | all-gather | bytes 479232 | tf_op jit(solution)/shard_map/all_gather | solution.py:213
  47.8 0.2 reshape.33.half
  48.0 7.1 %collective-permute-start.1 = (bf16[48,4608]{1,0:T(8,128)(2,1)S(1)}, bf16[48,4608]{1,0:T(8,128)(2,1)S(1)}, u32[]{:S(2)}, u32[]{:S(2)}) collective-permute-start(bf16[48,4608]{1,0:T(8,128)(2,1)S(1)} %reshape.33.half), channel_id=1, source_target_pairs={{0,1},{1,0},{2,3},{3,2},{4,5},{5,4},{6,7},{7,6},{8,9},{9,8},{10,11... | collective-permute-start | bytes 1327112 | tf_op jit(solution)/shard_map/ppermute | solution.py:215
  55.1 0.1 pad_add_fusion.place.refs_0_
  55.2 0.0 all-to-all-done.tg
  55.2 0.0 copy-done.2
  55.2 1.7 %shard_map.140 = (bf16[128,4096]{1,0:T(8,128)(2,1)S(1)}, f32[32,8,128]{2,1,0:T(8,128)S(1)}) custom-call(bf16[32,128,128]{2,1,0:T(8,128)(2,1)S(1)} %all-to-all-done.tg, bf16[128,4096]{1,0:T(8,128)(2,1)S(1)} %bitcast.18, f32[128,128]{1,0:T(8,128)S(1)} %get-tuple-element.21.cos, f32[128,128]{1,0:T(8,128)S(1)} %get-tuple-element.22.sin, ...), custom_call_target="tpu_custom_call" | custom-call | tf_op jit(solution)/shard_map/pallas_call | solution.py:237
  56.8 0.0 collective-permute-done.1.other
  56.9 2.4 %shard_map.141 = (f32[32,56,128]{2,1,0:T(8,128)S(1)}, bf16[32,56,128]{2,1,0:T(8,128)(2,1)S(1)}) custom-call(s32[3]{0:T(128)S(1)} %pad_add_fusion.place.refs_0_, bf16[128,5120]{1,0:T(8,128)(2,1)S(1)} %bitcast.19, bf16[48,4608]{1,0:T(8,128)(2,1)S(1)} %reshape.33.half, bf16[48,4608]{1,0:T(8,128)(2,1)S(1)} %collective-permute-done.1.other, ...), custom_call_target="tpu_custom_call" | custom-call | tf_op jit(solution)/shard_map/pallas_call | solution.py:248
  59.3 1.9 %collective-permute-start.2 = (bf16[32,56,128]{2,1,0:T(8,128)(2,1)S(1)}, bf16[32,56,128]{2,1,0:T(8,128)(2,1)S(1)}, u32[]{:S(2)}, u32[]{:S(2)}) collective-permute-start(bf16[32,56,128]{2,1,0:T(8,128)(2,1)S(1)} %get-tuple-element.27), channel_id=1, source_target_pairs={{0,1},{1,0},{2,3},{3,2},{4,5},{5,4},{6,7},{7,6},{8,9},{9,8},{10,11... | collective-permute-start | bytes 1376264 | tf_op jit(solution)/shard_map/ppermute | solution.py:259
  61.2 1.8 %collective-permute-done.2 = bf16[32,56,128]{2,1,0:T(8,128)(2,1)S(1)} collective-permute-done((bf16[32,56,128]{2,1,0:T(8,128)(2,1)S(1)}, bf16[32,56,128]{2,1,0:T(8,128)(2,1)S(1)}, u32[]{:S(2)}, u32[]{:S(2)}) %collective-permute-start.2) | collective-permute-done | bytes 458784 | tf_op jit(solution)/shard_map/ppermute | solution.py:259
  63.0 0.1 add_convert_fusion
  63.1 26.0 %all_to_all.20.refs_1_ = bf16[32,56,128]{2,1,0:T(8,128)(2,1)S(1)} all-to-all(bf16[32,56,128]{2,1,0:T(8,128)(2,1)S(1)} %add_convert_fusion), channel_id=1, replica_groups={{0,2,4,6,8,10,12,14,16,18,20,22,24,26,28,30,32,34,36,38,40,42,44,46,48,..., dimensions={0} | all-to-all | bytes 917504 | tf_op jit(solution)/shard_map/all_to_all | solution.py:267
  89.1 0.8 shard_map.142
  89.9 12.5 %all_to_all.21 = f32[12,8,128]{2,1,0:T(8,128)S(1)} all-to-all(f32[12,8,128]{2,1,0:T(8,128)S(1)} %bitcast.20), channel_id=1, replica_groups={{0,64,128,192,256,320,384,448,512,576,640,704},{32,96,160,224,288,352,4..., dimensions={0} | all-to-all | bytes 98304 | tf_op jit(solution)/shard_map/all_to_all | solution.py:277
  102.5 15.8 %all_to_all.22.refs_0_ = f32[32,8,128]{2,1,0:T(8,128)S(1)} all-to-all(f32[32,8,128]{2,1,0:T(8,128)S(1)} %broadcast_in_dim.58), channel_id=1, replica_groups=mesh['dp'=24,'seq'=32] {'seq'}, dimensions={0} | all-to-all | bytes 262144 | tf_op jit(solution)/shard_map/all_to_all | solution.py:279
  118.3 0.7 shard_map.143
  (18 shorter events, 0.1 us)
Async XLA Ops:
  0.6 16.4 %copy-start.7 = (f32[128]{0:T(128)S(1)}, f32[128]{0:T(128)}, u32[]{:S(2)}) copy-start(f32[128]{0:T(128)} %constant.51.clone) | copy-start | bytes 1540
  0.6 16.4 %copy-start.8 = (f32[128]{0:T(128)S(1)}, f32[128]{0:T(128)}, u32[]{:S(2)}) copy-start(f32[128]{0:T(128)} %constant.50.clone) | copy-start | bytes 1540
  0.7 16.4 %copy-start.9 = (pred[128]{0:T(512)(128)(4,1)S(1)}, pred[128]{0:T(512)(128)(4,1)}, u32[]{:S(2)}) copy-start(pred[128]{0:T(512)(128)(4,1)} %constant.49.clone) | copy-start | bytes 388
  0.7 16.4 %copy-start.10 = (pred[128]{0:T(512)(128)(4,1)S(1)}, pred[128]{0:T(512)(128)(4,1)}, u32[]{:S(2)}) copy-start(pred[128]{0:T(512)(128)(4,1)} %constant.48.clone) | copy-start | bytes 388
  0.7 14.3 %copy-start.5 = (bf16[1,2,4096]{2,1,0:T(2,128)(2,1)S(1)}, bf16[1,2,4096]{2,1,0:T(2,128)(2,1)}, u32[]{:S(2)}) copy-start(bf16[1,2,4096]{2,1,0:T(2,128)(2,1)} %param.16) | copy-start | bytes 49156
  0.7 14.3 %copy-start.4 = (bf16[1,2,5120]{2,1,0:T(2,128)(2,1)S(1)}, bf16[1,2,5120]{2,1,0:T(2,128)(2,1)}, u32[]{:S(2)}) copy-start(bf16[1,2,5120]{2,1,0:T(2,128)(2,1)} %param.15) | copy-start | bytes 61444
  0.7 16.2 %copy-start.6 = (s32[3,1,128]{2,1,0:T(1,128)S(1)}, s32[3,1,128]{2,1,0:T(1,128)}, u32[]{:S(2)}) copy-start(s32[3,1,128]{2,1,0:T(1,128)} %param.18) | copy-start | bytes 4612
  0.7 16.3 %copy-start.3 = (s32[1,128]{1,0:T(1,128)S(1)}, s32[1,128]{1,0:T(1,128)}, u32[]{:S(2)}) copy-start(s32[1,128]{1,0:T(1,128)} %valid.1) | copy-start | bytes 1540
  0.7 16.7 %copy-start = (bf16[1,1,128,4096]{3,2,1,0:T(8,128)(2,1)S(1)}, bf16[1,1,128,4096]{3,2,1,0:T(8,128)(2,1)}, u32[]{:S(2)}) copy-start(bf16[1,1,128,4096]{3,2,1,0:T(8,128)(2,1)} %param.12) | copy-start | bytes 3145732
  0.7 54.4 %all-to-all-start = ((bf16[32,128,128]{2,1,0:T(8,128)(2,1)}), bf16[32,128,128]{2,1,0:T(8,128)(2,1)S(1)}, u32[]{:S(2)}, u32[]{:S(2)}) async-start(bf16[32,128,128]{2,1,0:T(8,128)(2,1)} %bitcast.21), calls=%async_computation | async-start | bytes 2097152 | tf_op jit(solution)/shard_map/all_to_all | solution.py:226
  15.0 6.7 %collective-permute-start = (bf16[1,2,4608]{2,1,0:T(2,128)(2,1)S(1)}, bf16[1,2,4608]{2,1,0:T(2,128)(2,1)S(1)}, u32[]{:S(2)}, u32[]{:S(2)}) collective-permute-start(bf16[1,2,4608]{2,1,0:T(2,128)(2,1)S(1)} %broadcast_select_fusion), channel_id=1, source_target_pairs={{0,32},{32,0},{64,96},{96,64},{128,160},{160,128},{192,224},{224,1... | collective-permute-start | bytes 55304 | tf_op jit(solution)/shard_map/ppermute | solution.py:209
  17.4 37.8 %copy-start.2 = (f32[1,4096]{1,0:T(1,128)S(1)}, f32[1,4096]{1,0:T(1,128)}, u32[]{:S(2)}) copy-start(f32[1,4096]{1,0:T(1,128)} %gains.1) | copy-start | bytes 49156
  48.0 8.8 %collective-permute-start.1 = (bf16[48,4608]{1,0:T(8,128)(2,1)S(1)}, bf16[48,4608]{1,0:T(8,128)(2,1)S(1)}, u32[]{:S(2)}, u32[]{:S(2)}) collective-permute-start(bf16[48,4608]{1,0:T(8,128)(2,1)S(1)} %reshape.33.half), channel_id=1, source_target_pairs={{0,1},{1,0},{2,3},{3,2},{4,5},{5,4},{6,7},{7,6},{8,9},{9,8},{10,11... | collective-permute-start | bytes 1327112 | tf_op jit(solution)/shard_map/ppermute | solution.py:215
  55.2 1.7 %copy-start.1 = (bf16[1,128,5120]{2,1,0:T(8,128)(2,1)S(1)}, bf16[1,128,5120]{2,1,0:T(8,128)(2,1)}, u32[]{:S(2)}) copy-start(bf16[1,128,5120]{2,1,0:T(8,128)(2,1)} %param.17) | copy-start | bytes 3932164
  59.3 3.7 %collective-permute-start.2 = (bf16[32,56,128]{2,1,0:T(8,128)(2,1)S(1)}, bf16[32,56,128]{2,1,0:T(8,128)(2,1)S(1)}, u32[]{:S(2)}, u32[]{:S(2)}) collective-permute-start(bf16[32,56,128]{2,1,0:T(8,128)(2,1)S(1)} %get-tuple-element.27), channel_id=1, source_target_pairs={{0,1},{1,0},{2,3},{3,2},{4,5},{5,4},{6,7},{7,6},{8,9},{9,8},{10,11... | collective-permute-start | bytes 1376264 | tf_op jit(solution)/shard_map/ppermute | solution.py:259

commit v2 on v1

--- a/solution.py
+++ b/solution.py
@@ -99,12 +99,12 @@
     lax.fori_loop(0, tokens // (8 * group), some, 0)
 
 
-def sums_kernel(place, act, half, other, delta, gain, valid, mine, theirs, maps):
+def sums_kernel(act, half, other, delta, gain, valid, mine, theirs, maps):
     heads = gain.shape[0]
     ranks, cut = half.shape
     width = act.shape[1]
     each, quarter = ranks // 2, ranks // 8
-    c, hi = place[0], place[2]
+    c, hi = lax.axis_index("seq") % 2, lax.axis_index("dp") % 2
 
     @pl.when(c == 0)
     def _():
@@ -120,15 +120,16 @@
         return pl.ds(pl.multiple_of(tile * HD, HD), count * HD)
 
     r, k = onto((ranks, ranks), 0), onto((ranks, ranks), 1)
-    loc = r % each
-    order = (k == 4 * (loc // 2) + 2 * ((r // each) ^ hi) + loc % 2).astype(F32).astype(BF16)
+    far = (r >= each).astype(jnp.int32)
+    loc = r - each * far
+    order = (k == 2 * loc - (loc & 1) + 2 * (far ^ hi)).astype(F32).astype(BF16)
     up = nt(maps[:, 0:width], act[...]).astype(BF16)
     back = nt(maps[:, width:], delta[...]).astype(BF16)
     up = nn(order, up).astype(BF16)
     back = nn(order, back).astype(BF16)
     r, k = onto((8 * REM, ranks), 0), onto((8 * REM, ranks), 1)
-    at = (r // REM % 2) * each + (r // (2 * REM)) * quarter + r % REM
-    pick = ((k == at) & (r % REM < quarter)).astype(F32).astype(BF16)
+    at = ((r >> 3) & 1) * each + (r >> 4) * quarter + (r & 7)
+    pick = ((k == at) & ((r & 7) < quarter)).astype(F32).astype(BF16)
     rems = nn(pick, back).astype(BF16)
     count = jnp.sum(valid[...].astype(F32))
     row = onto((REM, HD), 0)
@@ -158,21 +159,22 @@
     lax.fori_loop(0, heads // 4, four, 0, unroll=4)
 
 
-def spread_kernel(place, blocks, out, total, ranks, length):
+def spread_kernel(blocks, out, total, ranks, length):
     peers, rows, _ = blocks.shape
     acc = blocks[0].astype(F32)
     for i in range(1, peers):
         acc = acc + blocks[i].astype(F32)
     total[...] = jnp.zeros_like(total)
     total[0:rows, :] = acc
-    q = place[1]
+    q = lax.axis_index("seq") % 4
     quarter = ranks // 4
     shape = (8 * length, total.shape[0])
     r, k = onto(shape, 0), onto(shape, 1)
-    j = r % 8
-    at = 2 * (r // 8) + j % 2
+    j = r & 7
+    at = 2 * (r >> 3) + (j & 1)
     want = jnp.where(j < 2, at, at + ranks)
-    rem = jnp.where(at // quarter == q, 2 * ranks + at % quarter, -1)
+    rem = at - quarter * q
+    rem = jnp.where((rem >= 0) & (rem < quarter), 2 * ranks + rem, -1)
     want = jnp.where(j < 4, want, rem)
     want = jnp.where(j < 6, want, 2 * ranks + quarter + j - 6)
     pick = (k == want).astype(F32)
@@ -195,7 +197,6 @@
 
 
 VMEM = pl.BlockSpec(memory_space=pltpu.VMEM)
-SMEM = pl.BlockSpec(memory_space=pltpu.SMEM)
 
 
 def within(mib):
@@ -233,7 +234,6 @@
     )(proj, *rope_tables(positions[:, 0], valid[0]))
     half, other, tables = gather_ranks(adapter_lowering, adapter_raising, dp, seq, member, tables)
     rows = ranks + REM
-    place = jnp.stack([member % 2, member % 4, lax.axis_index("dp") % 2]).astype(jnp.int32)
     delta, gain = pl.pallas_call(
         delta_kernel,
         out_shape=(
@@ -251,11 +251,11 @@
             jax.ShapeDtypeStruct((seq, rows, HD), F32),
             jax.ShapeDtypeStruct((seq, rows, HD), BF16),
         ),
-        in_specs=[SMEM] + [VMEM] * 6,
+        in_specs=[VMEM] * 6,
         out_specs=(VMEM, VMEM),
         compiler_params=within(8),
         scratch_shapes=[pltpu.VMEM((ranks, act.shape[1] + features), BF16)],
-    )(place, act, half, other, delta, gain, valid)
+    )(act, half, other, delta, gain, valid)
     partner = lax.ppermute(theirs, "seq", [(s, s ^ 1) for s in range(seq)])
     both = (mine + partner.astype(F32)).astype(BF16)
     length = dp // 2
@@ -268,11 +268,11 @@
     rank_rows = pl.pallas_call(
         lambda *refs: spread_kernel(*refs, ranks=ranks // 2, length=length),
         out_shape=jax.ShapeDtypeStruct((8 * length, HD), F32),
-        in_specs=[SMEM, VMEM],
+        in_specs=[VMEM],
         out_specs=VMEM,
         compiler_params=within(4),
         scratch_shapes=[pltpu.VMEM((128, HD), F32)],
-    )(place, blocks)
+    )(blocks)
     along_z = [list(range(hi, dp, 2)) for hi in range(2)]
     shares = lax.all_to_all(rank_rows.reshape(length, 8, HD), "dp", 0, 0, tiled=True, axis_index_groups=along_z)
     share = jnp.sum(shares, axis=0)

time: 119 us -> 118 us (level)
  no operation moved by 1% of the time
where the time goes in v2:
time: 118 us
  blocking collectives  80.3 us (68%)
  starting transfers between devices  25.1 us (21%)
  waiting for transfers between devices  5.67 us (5%)
  Pallas kernels  4.93 us (4%)
    all_gather x1, blocking collectives, gather_ranks(): lax.all_gather(pair, 'dp', axis=0, tiled=True, axis_index_groups=along_z)  26 us
    all_to_all x1, blocking collectives, shards(): lax.all_to_all(both, ('dp', 'seq'), 0, 0, tiled=True, axis_index_groups=p...  26 us
    all_to_all x1, blocking collectives, shards(): lax.all_to_all(jnp.broadcast_to(share, (seq, 8, HD)), 'seq', 0, 0, tiled=...  15.8 us
    all_to_all x1, starting transfers between devices, shards(): tg = lax.all_to_all(tg, 'seq', 0, 0, tiled=True)  14.2 us
    all_to_all x1, blocking collectives, shards(): lax.all_to_all(rank_rows.reshape(length, 8, HD), 'dp', 0, 0, tiled=True,...  12.5 us
    ppermute x1, starting transfers between devices, gather_ranks(): other = lax.ppermute(half, 'seq', [(s, s ^ 1) for s in range(seq)])  7.06 us
    ppermute x1, waiting for transfers between devices, gather_ranks(): near = lax.ppermute(own, 'dp', [(d, d ^ 1) for d in range(dp)])  3.9 us
  transfers between devices with their start and end apart: 4, of which 2 were waited for; matrix products, arithmetic and copies ran while one was open for 1% of the time, Pallas kernels for 2%

profile of v2, /device:TPU:1, one launch (start us, length us, event | category | flops | bytes accessed | tf_op | source)
XLA Modules:
  0.0 117.8 jit_solution(17529254234482218387)
XLA Ops:
  0.6 0.0 copy-start.7
  0.6 0.0 copy-start.8
  0.7 0.0 copy-start.9
  0.7 0.0 copy-start.10
  0.7 0.0 copy-start.5
  0.7 0.0 copy-start.4
  0.7 0.0 copy-start.6
  0.7 0.0 copy-start.3
  0.7 14.2 %all-to-all-start = ((bf16[32,128,128]{2,1,0:T(8,128)(2,1)}), bf16[32,128,128]{2,1,0:T(8,128)(2,1)S(1)}, u32[]{:S(2)}, u32[]{:S(2)}) async-start(bf16[32,128,128]{2,1,0:T(8,128)(2,1)} %bitcast.18), calls=%async_computation | async-start | bytes 2097152 | tf_op jit(solution)/shard_map/all_to_all | solution.py:227
  15.0 1.9 %collective-permute-start = (bf16[1,2,4608]{2,1,0:T(2,128)(2,1)S(1)}, bf16[1,2,4608]{2,1,0:T(2,128)(2,1)S(1)}, u32[]{:S(2)}, u32[]{:S(2)}) collective-permute-start(bf16[1,2,4608]{2,1,0:T(2,128)(2,1)S(1)} %broadcast_select_fusion), channel_id=1, source_target_pairs={{0,32},{32,0},{64,96},{96,64},{128,160},{160,128},{192,224},{224,1... | collective-permute-start | bytes 55304 | tf_op jit(solution)/shard_map/ppermute | solution.py:210
  17.0 0.4 multiply_multiply_fusion
  17.4 0.0 copy-start.2
  17.4 0.4 shard_map.139
  17.9 3.9 %collective-permute-done = bf16[1,2,4608]{2,1,0:T(2,128)(2,1)S(1)} collective-permute-done((bf16[1,2,4608]{2,1,0:T(2,128)(2,1)S(1)}, bf16[1,2,4608]{2,1,0:T(2,128)(2,1)S(1)}, u32[]{:S(2)}, u32[]{:S(2)}) %collective-permute-start) | collective-permute-done | bytes 18464 | tf_op jit(solution)/shard_map/ppermute | solution.py:210
  21.8 0.1 pad_maximum_fusion
  21.8 26.0 %all_gather.3 = bf16[24,2,4608]{2,1,0:T(2,128)(2,1)S(1)} all-gather(bf16[2,2,4608]{2,1,0:T(2,128)(2,1)S(1)} %pad_maximum_fusion), channel_id=1, replica_groups={{0,64,128,192,256,320,384,448,512,576,640,704},{32,96,160,224,288,352,4..., dimensions={0}, use_global_device_ids=true | all-gather | bytes 479232 | tf_op jit(solution)/shard_map/all_gather | solution.py:214
  47.8 0.2 reshape.33.half
  48.0 7.1 %collective-permute-start.1 = (bf16[48,4608]{1,0:T(8,128)(2,1)S(1)}, bf16[48,4608]{1,0:T(8,128)(2,1)S(1)}, u32[]{:S(2)}, u32[]{:S(2)}) collective-permute-start(bf16[48,4608]{1,0:T(8,128)(2,1)S(1)} %reshape.33.half), channel_id=1, source_target_pairs={{0,1},{1,0},{2,3},{3,2},{4,5},{5,4},{6,7},{7,6},{8,9},{9,8},{10,11... | collective-permute-start | bytes 1327112 | tf_op jit(solution)/shard_map/ppermute | solution.py:216
  55.1 0.0 all-to-all-done.tg
  55.1 0.0 copy-done.2
  55.1 0.0 copy-start.1
  55.1 1.7 %shard_map.140 = (bf16[128,4096]{1,0:T(8,128)(2,1)S(1)}, f32[32,8,128]{2,1,0:T(8,128)S(1)}) custom-call(bf16[32,128,128]{2,1,0:T(8,128)(2,1)S(1)} %all-to-all-done.tg, bf16[128,4096]{1,0:T(8,128)(2,1)S(1)} %bitcast.15, f32[128,128]{1,0:T(8,128)S(1)} %get-tuple-element.21.cos, f32[128,128]{1,0:T(8,128)S(1)} %get-tuple-element.22.sin, ...), custom_call_target="tpu_custom_call" | custom-call | tf_op jit(solution)/shard_map/pallas_call | solution.py:237
  56.8 0.0 collective-permute-done.1.other
  56.8 1.9 %shard_map.141 = (f32[32,56,128]{2,1,0:T(8,128)S(1)}, bf16[32,56,128]{2,1,0:T(8,128)(2,1)S(1)}) custom-call(bf16[128,5120]{1,0:T(8,128)(2,1)S(1)} %bitcast.16, bf16[48,4608]{1,0:T(8,128)(2,1)S(1)} %reshape.33.half, bf16[48,4608]{1,0:T(8,128)(2,1)S(1)} %collective-permute-done.1.other, bf16[128,4096]{1,0:T(8,128)(2,1)S(1)} %get-tuple-element.24.delta, ...), custom_call_target="tpu_custom_call" | custom-call | tf_op jit(solution)/shard_map/pallas_call | solution.py:248
  58.7 1.9 %collective-permute-start.2 = (bf16[32,56,128]{2,1,0:T(8,128)(2,1)S(1)}, bf16[32,56,128]{2,1,0:T(8,128)(2,1)S(1)}, u32[]{:S(2)}, u32[]{:S(2)}) collective-permute-start(bf16[32,56,128]{2,1,0:T(8,128)(2,1)S(1)} %get-tuple-element.27), channel_id=1, source_target_pairs={{0,1},{1,0},{2,3},{3,2},{4,5},{5,4},{6,7},{7,6},{8,9},{9,8},{10,11... | collective-permute-start | bytes 1376264 | tf_op jit(solution)/shard_map/ppermute | solution.py:259
  60.6 1.8 %collective-permute-done.2 = bf16[32,56,128]{2,1,0:T(8,128)(2,1)S(1)} collective-permute-done((bf16[32,56,128]{2,1,0:T(8,128)(2,1)S(1)}, bf16[32,56,128]{2,1,0:T(8,128)(2,1)S(1)}, u32[]{:S(2)}, u32[]{:S(2)}) %collective-permute-start.2) | collective-permute-done | bytes 458784 | tf_op jit(solution)/shard_map/ppermute | solution.py:259
  62.4 0.1 add_convert_fusion
  62.5 26.0 %all_to_all.20.refs_0_ = bf16[32,56,128]{2,1,0:T(8,128)(2,1)S(1)} all-to-all(bf16[32,56,128]{2,1,0:T(8,128)(2,1)S(1)} %add_convert_fusion), channel_id=1, replica_groups={{0,2,4,6,8,10,12,14,16,18,20,22,24,26,28,30,32,34,36,38,40,42,44,46,48,..., dimensions={0} | all-to-all | bytes 917504 | tf_op jit(solution)/shard_map/all_to_all | solution.py:267
  88.5 0.3 shard_map.142
  88.8 12.5 %all_to_all.21 = f32[12,8,128]{2,1,0:T(8,128)S(1)} all-to-all(f32[12,8,128]{2,1,0:T(8,128)S(1)} %bitcast.17), channel_id=1, replica_groups={{0,64,128,192,256,320,384,448,512,576,640,704},{32,96,160,224,288,352,4..., dimensions={0} | all-to-all | bytes 98304 | tf_op jit(solution)/shard_map/all_to_all | solution.py:277
  101.3 15.8 %all_to_all.22.refs_0_ = f32[32,8,128]{2,1,0:T(8,128)S(1)} all-to-all(f32[32,8,128]{2,1,0:T(8,128)S(1)} %broadcast_in_dim.58), channel_id=1, replica_groups=mesh['dp'=24,'seq'=32] {'seq'}, dimensions={0} | all-to-all | bytes 262144 | tf_op jit(solution)/shard_map/all_to_all | solution.py:279
  117.1 0.7 shard_map.143
  (17 shorter events, 0.1 us)
Async XLA Ops:
  0.6 16.4 %copy-start.7 = (f32[128]{0:T(128)S(1)}, f32[128]{0:T(128)}, u32[]{:S(2)}) copy-start(f32[128]{0:T(128)} %constant.31.clone) | copy-start | bytes 1540
  0.6 16.4 %copy-start.8 = (f32[128]{0:T(128)S(1)}, f32[128]{0:T(128)}, u32[]{:S(2)}) copy-start(f32[128]{0:T(128)} %constant.30.clone) | copy-start | bytes 1540
  0.7 16.4 %copy-start.9 = (pred[128]{0:T(512)(128)(4,1)S(1)}, pred[128]{0:T(512)(128)(4,1)}, u32[]{:S(2)}) copy-start(pred[128]{0:T(512)(128)(4,1)} %constant.29.clone) | copy-start | bytes 388
  0.7 16.4 %copy-start.10 = (pred[128]{0:T(512)(128)(4,1)S(1)}, pred[128]{0:T(512)(128)(4,1)}, u32[]{:S(2)}) copy-start(pred[128]{0:T(512)(128)(4,1)} %constant.28.clone) | copy-start | bytes 388
  0.7 14.3 %copy-start.5 = (bf16[1,2,4096]{2,1,0:T(2,128)(2,1)S(1)}, bf16[1,2,4096]{2,1,0:T(2,128)(2,1)}, u32[]{:S(2)}) copy-start(bf16[1,2,4096]{2,1,0:T(2,128)(2,1)} %param.16) | copy-start | bytes 49156
  0.7 14.3 %copy-start.4 = (bf16[1,2,5120]{2,1,0:T(2,128)(2,1)S(1)}, bf16[1,2,5120]{2,1,0:T(2,128)(2,1)}, u32[]{:S(2)}) copy-start(bf16[1,2,5120]{2,1,0:T(2,128)(2,1)} %param.15) | copy-start | bytes 61444
  0.7 16.2 %copy-start.6 = (s32[3,1,128]{2,1,0:T(1,128)S(1)}, s32[3,1,128]{2,1,0:T(1,128)}, u32[]{:S(2)}) copy-start(s32[3,1,128]{2,1,0:T(1,128)} %param.18) | copy-start | bytes 4612
  0.7 16.3 %copy-start.3 = (s32[1,128]{1,0:T(1,128)S(1)}, s32[1,128]{1,0:T(1,128)}, u32[]{:S(2)}) copy-start(s32[1,128]{1,0:T(1,128)} %valid.1) | copy-start | bytes 1540
  0.7 16.7 %copy-start = (bf16[1,1,128,4096]{3,2,1,0:T(8,128)(2,1)S(1)}, bf16[1,1,128,4096]{3,2,1,0:T(8,128)(2,1)}, u32[]{:S(2)}) copy-start(bf16[1,1,128,4096]{3,2,1,0:T(8,128)(2,1)} %param.12) | copy-start | bytes 3145732
  0.7 54.3 %all-to-all-start = ((bf16[32,128,128]{2,1,0:T(8,128)(2,1)}), bf16[32,128,128]{2,1,0:T(8,128)(2,1)S(1)}, u32[]{:S(2)}, u32[]{:S(2)}) async-start(bf16[32,128,128]{2,1,0:T(8,128)(2,1)} %bitcast.18), calls=%async_computation | async-start | bytes 2097152 | tf_op jit(solution)/shard_map/all_to_all | solution.py:227
  15.0 6.7 %collective-permute-start = (bf16[1,2,4608]{2,1,0:T(2,128)(2,1)S(1)}, bf16[1,2,4608]{2,1,0:T(2,128)(2,1)S(1)}, u32[]{:S(2)}, u32[]{:S(2)}) collective-permute-start(bf16[1,2,4608]{2,1,0:T(2,128)(2,1)S(1)} %broadcast_select_fusion), channel_id=1, source_target_pairs={{0,32},{32,0},{64,96},{96,64},{128,160},{160,128},{192,224},{224,1... | collective-permute-start | bytes 55304 | tf_op jit(solution)/shard_map/ppermute | solution.py:210
  17.4 37.7 %copy-start.2 = (f32[1,4096]{1,0:T(1,128)S(1)}, f32[1,4096]{1,0:T(1,128)}, u32[]{:S(2)}) copy-start(f32[1,4096]{1,0:T(1,128)} %gains.1) | copy-start | bytes 49156
  48.0 8.8 %collective-permute-start.1 = (bf16[48,4608]{1,0:T(8,128)(2,1)S(1)}, bf16[48,4608]{1,0:T(8,128)(2,1)S(1)}, u32[]{:S(2)}, u32[]{:S(2)}) collective-permute-start(bf16[48,4608]{1,0:T(8,128)(2,1)S(1)} %reshape.33.half), channel_id=1, source_target_pairs={{0,1},{1,0},{2,3},{3,2},{4,5},{5,4},{6,7},{7,6},{8,9},{9,8},{10,11... | collective-permute-start | bytes 1327112 | tf_op jit(solution)/shard_map/ppermute | solution.py:216
  55.1 1.7 %copy-start.1 = (bf16[1,128,5120]{2,1,0:T(8,128)(2,1)S(1)}, bf16[1,128,5120]{2,1,0:T(8,128)(2,1)}, u32[]{:S(2)}) copy-start(bf16[1,128,5120]{2,1,0:T(8,128)(2,1)} %param.17) | copy-start | bytes 3932164
  58.7 3.7 %collective-permute-start.2 = (bf16[32,56,128]{2,1,0:T(8,128)(2,1)S(1)}, bf16[32,56,128]{2,1,0:T(8,128)(2,1)S(1)}, u32[]{:S(2)}, u32[]{:S(2)}) collective-permute-start(bf16[32,56,128]{2,1,0:T(8,128)(2,1)S(1)} %get-tuple-element.27), channel_id=1, source_target_pairs={{0,1},{1,0},{2,3},{3,2},{4,5},{5,4},{6,7},{7,6},{8,9},{9,8},{10,11... | collective-permute-start | bytes 1376264 | tf_op jit(solution)/shard_map/ppermute | solution.py:259

commit v3 on v2

--- a/solution.py
+++ b/solution.py
@@ -105,13 +105,14 @@
     width = act.shape[1]
     each, quarter = ranks // 2, ranks // 8
     c, hi = lax.axis_index("seq") % 2, lax.axis_index("dp") % 2
-
-    @pl.when(c == 0)
+    part = (lax.axis_index("seq") + lax.axis_index("dp") // 2) % 2
+
+    @pl.when(part == 0)
     def _():
         maps[:, 0:cut] = half[...]
         maps[:, cut:] = other[...]
 
-    @pl.when(c != 0)
+    @pl.when(part != 0)
     def _():
         maps[:, 0:cut] = other[...]
         maps[:, cut:] = half[...]
@@ -206,12 +207,18 @@
 def gather_ranks(adapter_lowering, adapter_raising, dp, seq, member, small):
     own = jnp.concatenate([adapter_lowering, adapter_raising], axis=2)
     cut = own.shape[2] // 2
-    own = jnp.where(member % 2 == 0, own[:, :, :cut], own[:, :, cut:])
+    part = (member + lax.axis_index("dp") // 2) % 2
+    own = jnp.where(part == 0, own[:, :, :cut], own[:, :, cut:])
     near = lax.ppermute(own, "dp", [(d, d ^ 1) for d in range(dp)])
     pair = jnp.concatenate([own, near], axis=0)
     pair, small = lax.optimization_barrier((pair, small))
-    along_z = [list(range(hi, dp, 2)) for hi in range(2)]
-    half = lax.all_gather(pair, "dp", axis=0, tiled=True, axis_index_groups=along_z)
+    rings = [
+        [(2 * z + hi) * seq + chip + (first + z) % 2 for z in range(dp // 2)]
+        for hi in range(2)
+        for chip in range(0, seq, 2)
+        for first in range(2)
+    ]
+    half = lax.all_gather(pair, ("dp", "seq"), axis=0, tiled=True, axis_index_groups=rings)
     half = half.reshape(dp * own.shape[1], cut)
     other = lax.ppermute(half, "seq", [(s, s ^ 1) for s in range(seq)])
     return half, other, small

time: 118 us -> 117 us (level)
  starting transfers between devices: 25.1 us -> 20.4 us
  blocking collectives: 80.3 us -> 83.8 us
    ppermute x1, starting transfers between devices: 7.06 us -> 1.92 us  [gather_ranks(): other = lax.ppermute(half, 'seq', [(s, s ^ 1) for s in range(seq)])]
    all_gather x1, blocking collectives: 26 us -> 28.5 us  [gather_ranks(): lax.all_gather(pair, ('dp', 'seq'), axis=0, tiled=True, axis_index_groups...]
  transfers between devices with their start and end apart: 4 -> 4, of which waited for: 2 -> 3; matrix products, arithmetic and copies ran while one was open for 1% -> 1% of each run, Pallas kernels for 2% -> 2%
where the time goes in v3:
time: 117 us; the launch traced here: 116 us
  blocking collectives  83.8 us (72%)
  starting transfers between devices  20.4 us (17%)
  waiting for transfers between devices  5.41 us (5%)
  Pallas kernels  4.94 us (4%)
    all_gather x1, blocking collectives, gather_ranks(): lax.all_gather(pair, ('dp', 'seq'), axis=0, tiled=True, axis_index_groups...  28.5 us
    all_to_all x1, blocking collectives, shards(): lax.all_to_all(both, ('dp', 'seq'), 0, 0, tiled=True, axis_index_groups=p...  26.4 us
    all_to_all x1, blocking collectives, shards(): lax.all_to_all(jnp.broadcast_to(share, (seq, 8, HD)), 'seq', 0, 0, tiled=...  16.1 us
    all_to_all x1, starting transfers between devices, shards(): tg = lax.all_to_all(tg, 'seq', 0, 0, tiled=True)  14.2 us
    all_to_all x1, blocking collectives, shards(): lax.all_to_all(rank_rows.reshape(length, 8, HD), 'dp', 0, 0, tiled=True,...  12.8 us
    ppermute x1, waiting for transfers between devices, gather_ranks(): near = lax.ppermute(own, 'dp', [(d, d ^ 1) for d in range(dp)])  3.92 us
    ppermute x1, starting transfers between devices, shards(): partner = lax.ppermute(theirs, 'seq', [(s, s ^ 1) for s in range(seq)])  2.4 us
  transfers between devices with their start and end apart: 4, of which 3 were waited for; matrix products, arithmetic and copies ran while one was open for 1% of the time, Pallas kernels for 2%

profile of v3, /device:TPU:1, one launch (start us, length us, event | category | flops | bytes accessed | tf_op | source)
XLA Modules:
  0.0 116.3 jit_solution(13103480684719304984)
XLA Ops:
  0.6 0.0 copy-start.7
  0.6 0.0 copy-start.8
  0.7 0.0 copy-start.9
  0.7 0.0 copy-start.10
  0.7 0.0 copy-start.5
  0.7 0.0 copy-start.4
  0.7 0.0 copy-start.6
  0.7 0.0 copy-start.3
  0.7 0.0 copy-start
  0.7 14.2 %all-to-all-start = ((bf16[32,128,128]{2,1,0:T(8,128)(2,1)}), bf16[32,128,128]{2,1,0:T(8,128)(2,1)S(1)}, u32[]{:S(2)}, u32[]{:S(2)}) async-start(bf16[32,128,128]{2,1,0:T(8,128)(2,1)} %bitcast.18), calls=%async_computation | async-start | bytes 2097152 | tf_op jit(solution)/shard_map/all_to_all | solution.py:234
  15.0 1.9 %collective-permute-start = (bf16[1,2,4608]{2,1,0:T(2,128)(2,1)S(1)}, bf16[1,2,4608]{2,1,0:T(2,128)(2,1)S(1)}, u32[]{:S(2)}, u32[]{:S(2)}) collective-permute-start(bf16[1,2,4608]{2,1,0:T(2,128)(2,1)S(1)} %broadcast_select_fusion), channel_id=1, source_target_pairs={{0,32},{32,0},{64,96},{96,64},{128,160},{160,128},{192,224},{224,1... | collective-permute-start | bytes 55304 | tf_op jit(solution)/shard_map/ppermute | solution.py:212
  17.1 0.4 multiply_multiply_fusion
  17.4 0.0 copy-start.2
  17.4 0.4 shard_map.139
  17.9 3.9 %collective-permute-done = bf16[1,2,4608]{2,1,0:T(2,128)(2,1)S(1)} collective-permute-done((bf16[1,2,4608]{2,1,0:T(2,128)(2,1)S(1)}, bf16[1,2,4608]{2,1,0:T(2,128)(2,1)S(1)}, u32[]{:S(2)}, u32[]{:S(2)}) %collective-permute-start) | collective-permute-done | bytes 18464 | tf_op jit(solution)/shard_map/ppermute | solution.py:212
  21.8 0.1 pad_maximum_fusion
  21.9 28.5 %all_gather.3 = bf16[24,2,4608]{2,1,0:T(2,128)(2,1)S(1)} all-gather(bf16[2,2,4608]{2,1,0:T(2,128)(2,1)S(1)} %pad_maximum_fusion), channel_id=1, replica_groups={{0,65,128,193,256,321,384,449,512,577,640,705},{1,64,129,192,257,320,38..., dimensions={0}, use_global_device_ids=true | all-gather | bytes 479232 | tf_op jit(solution)/shard_map/all_gather | solution.py:221
  50.3 0.2 reshape.33.half
  50.5 1.9 %collective-permute-start.1 = (bf16[48,4608]{1,0:T(8,128)(2,1)S(1)}, bf16[48,4608]{1,0:T(8,128)(2,1)S(1)}, u32[]{:S(2)}, u32[]{:S(2)}) collective-permute-start(bf16[48,4608]{1,0:T(8,128)(2,1)S(1)} %reshape.33.half), channel_id=1, source_target_pairs={{0,1},{1,0},{2,3},{3,2},{4,5},{5,4},{6,7},{7,6},{8,9},{9,8},{10,11... | collective-permute-start | bytes 1327112 | tf_op jit(solution)/shard_map/ppermute | solution.py:223
  52.4 0.0 all-to-all-done.tg
  52.5 0.0 copy-start.1
  52.5 1.7 %shard_map.140 = (bf16[128,4096]{1,0:T(8,128)(2,1)S(1)}, f32[32,8,128]{2,1,0:T(8,128)S(1)}) custom-call(bf16[32,128,128]{2,1,0:T(8,128)(2,1)S(1)} %all-to-all-done.tg, bf16[128,4096]{1,0:T(8,128)(2,1)S(1)} %bitcast.15, f32[128,128]{1,0:T(8,128)S(1)} %get-tuple-element.21.cos, f32[128,128]{1,0:T(8,128)S(1)} %get-tuple-element.22.sin, ...), custom_call_target="tpu_custom_call" | custom-call | tf_op jit(solution)/shard_map/pallas_call | solution.py:244
  54.1 0.1 collective-permute-done.1.other
  54.2 1.9 %shard_map.141 = (f32[32,56,128]{2,1,0:T(8,128)S(1)}, bf16[32,56,128]{2,1,0:T(8,128)(2,1)S(1)}) custom-call(bf16[128,5120]{1,0:T(8,128)(2,1)S(1)} %bitcast.16, bf16[48,4608]{1,0:T(8,128)(2,1)S(1)} %reshape.33.half, bf16[48,4608]{1,0:T(8,128)(2,1)S(1)} %collective-permute-done.1.other, bf16[128,4096]{1,0:T(8,128)(2,1)S(1)} %get-tuple-element.24.delta, ...), custom_call_target="tpu_custom_call" | custom-call | tf_op jit(solution)/shard_map/pallas_call | solution.py:255
  56.1 2.4 %collective-permute-start.2 = (bf16[32,56,128]{2,1,0:T(8,128)(2,1)S(1)}, bf16[32,56,128]{2,1,0:T(8,128)(2,1)S(1)}, u32[]{:S(2)}, u32[]{:S(2)}) collective-permute-start(bf16[32,56,128]{2,1,0:T(8,128)(2,1)S(1)} %get-tuple-element.27), channel_id=1, source_target_pairs={{0,1},{1,0},{2,3},{3,2},{4,5},{5,4},{6,7},{7,6},{8,9},{9,8},{10,11... | collective-permute-start | bytes 1376264 | tf_op jit(solution)/shard_map/ppermute | solution.py:266
  58.5 1.4 %collective-permute-done.2 = bf16[32,56,128]{2,1,0:T(8,128)(2,1)S(1)} collective-permute-done((bf16[32,56,128]{2,1,0:T(8,128)(2,1)S(1)}, bf16[32,56,128]{2,1,0:T(8,128)(2,1)S(1)}, u32[]{:S(2)}, u32[]{:S(2)}) %collective-permute-start.2) | collective-permute-done | bytes 458784 | tf_op jit(solution)/shard_map/ppermute | solution.py:266
  59.9 0.1 add_convert_fusion
  60.0 26.4 %all_to_all.20.refs_0_ = bf16[32,56,128]{2,1,0:T(8,128)(2,1)S(1)} all-to-all(bf16[32,56,128]{2,1,0:T(8,128)(2,1)S(1)} %add_convert_fusion), channel_id=1, replica_groups={{0,2,4,6,8,10,12,14,16,18,20,22,24,26,28,30,32,34,36,38,40,42,44,46,48,..., dimensions={0} | all-to-all | bytes 917504 | tf_op jit(solution)/shard_map/all_to_all | solution.py:274
  86.4 0.3 shard_map.142
  86.7 12.8 %all_to_all.21 = f32[12,8,128]{2,1,0:T(8,128)S(1)} all-to-all(f32[12,8,128]{2,1,0:T(8,128)S(1)} %bitcast.17), channel_id=1, replica_groups={{0,64,128,192,256,320,384,448,512,576,640,704},{32,96,160,224,288,352,4..., dimensions={0} | all-to-all | bytes 98304 | tf_op jit(solution)/shard_map/all_to_all | solution.py:284
  99.5 16.1 %all_to_all.22.refs_0_ = f32[32,8,128]{2,1,0:T(8,128)S(1)} all-to-all(f32[32,8,128]{2,1,0:T(8,128)S(1)} %broadcast_in_dim.58), channel_id=1, replica_groups=mesh['dp'=24,'seq'=32] {'seq'}, dimensions={0} | all-to-all | bytes 262144 | tf_op jit(solution)/shard_map/all_to_all | solution.py:286
  115.6 0.7 shard_map.143
  (17 shorter events, 0.1 us)
Async XLA Ops:
  0.6 16.4 %copy-start.7 = (f32[128]{0:T(128)S(1)}, f32[128]{0:T(128)}, u32[]{:S(2)}) copy-start(f32[128]{0:T(128)} %constant.46.clone) | copy-start | bytes 1540
  0.6 16.4 %copy-start.8 = (f32[128]{0:T(128)S(1)}, f32[128]{0:T(128)}, u32[]{:S(2)}) copy-start(f32[128]{0:T(128)} %constant.45.clone) | copy-start | bytes 1540
  0.7 16.4 %copy-start.9 = (pred[128]{0:T(512)(128)(4,1)S(1)}, pred[128]{0:T(512)(128)(4,1)}, u32[]{:S(2)}) copy-start(pred[128]{0:T(512)(128)(4,1)} %constant.44.clone) | copy-start | bytes 388
  0.7 16.4 %copy-start.10 = (pred[128]{0:T(512)(128)(4,1)S(1)}, pred[128]{0:T(512)(128)(4,1)}, u32[]{:S(2)}) copy-start(pred[128]{0:T(512)(128)(4,1)} %constant.43.clone) | copy-start | bytes 388
  0.7 14.3 %copy-start.5 = (bf16[1,2,4096]{2,1,0:T(2,128)(2,1)S(1)}, bf16[1,2,4096]{2,1,0:T(2,128)(2,1)}, u32[]{:S(2)}) copy-start(bf16[1,2,4096]{2,1,0:T(2,128)(2,1)} %param.16) | copy-start | bytes 49156
  0.7 14.3 %copy-start.4 = (bf16[1,2,5120]{2,1,0:T(2,128)(2,1)S(1)}, bf16[1,2,5120]{2,1,0:T(2,128)(2,1)}, u32[]{:S(2)}) copy-start(bf16[1,2,5120]{2,1,0:T(2,128)(2,1)} %param.15) | copy-start | bytes 61444
  0.7 16.3 %copy-start.6 = (s32[3,1,128]{2,1,0:T(1,128)S(1)}, s32[3,1,128]{2,1,0:T(1,128)}, u32[]{:S(2)}) copy-start(s32[3,1,128]{2,1,0:T(1,128)} %param.18) | copy-start | bytes 4612
  0.7 16.3 %copy-start.3 = (s32[1,128]{1,0:T(1,128)S(1)}, s32[1,128]{1,0:T(1,128)}, u32[]{:S(2)}) copy-start(s32[1,128]{1,0:T(1,128)} %valid.1) | copy-start | bytes 1540
  0.7 16.7 %copy-start = (bf16[1,1,128,4096]{3,2,1,0:T(8,128)(2,1)S(1)}, bf16[1,1,128,4096]{3,2,1,0:T(8,128)(2,1)}, u32[]{:S(2)}) copy-start(bf16[1,1,128,4096]{3,2,1,0:T(8,128)(2,1)} %param.12) | copy-start | bytes 3145732
  0.7 51.7 %all-to-all-start = ((bf16[32,128,128]{2,1,0:T(8,128)(2,1)}), bf16[32,128,128]{2,1,0:T(8,128)(2,1)S(1)}, u32[]{:S(2)}, u32[]{:S(2)}) async-start(bf16[32,128,128]{2,1,0:T(8,128)(2,1)} %bitcast.18), calls=%async_computation | async-start | bytes 2097152 | tf_op jit(solution)/shard_map/all_to_all | solution.py:234
  15.0 6.8 %collective-permute-start = (bf16[1,2,4608]{2,1,0:T(2,128)(2,1)S(1)}, bf16[1,2,4608]{2,1,0:T(2,128)(2,1)S(1)}, u32[]{:S(2)}, u32[]{:S(2)}) collective-permute-start(bf16[1,2,4608]{2,1,0:T(2,128)(2,1)S(1)} %broadcast_select_fusion), channel_id=1, source_target_pairs={{0,32},{32,0},{64,96},{96,64},{128,160},{160,128},{192,224},{224,1... | collective-permute-start | bytes 55304 | tf_op jit(solution)/shard_map/ppermute | solution.py:212
  17.4 35.0 %copy-start.2 = (f32[1,4096]{1,0:T(1,128)S(1)}, f32[1,4096]{1,0:T(1,128)}, u32[]{:S(2)}) copy-start(f32[1,4096]{1,0:T(1,128)} %gains.1) | copy-start | bytes 49156
  50.5 3.7 %collective-permute-start.1 = (bf16[48,4608]{1,0:T(8,128)(2,1)S(1)}, bf16[48,4608]{1,0:T(8,128)(2,1)S(1)}, u32[]{:S(2)}, u32[]{:S(2)}) collective-permute-start(bf16[48,4608]{1,0:T(8,128)(2,1)S(1)} %reshape.33.half), channel_id=1, source_target_pairs={{0,1},{1,0},{2,3},{3,2},{4,5},{5,4},{6,7},{7,6},{8,9},{9,8},{10,11... | collective-permute-start | bytes 1327112 | tf_op jit(solution)/shard_map/ppermute | solution.py:223
  52.5 1.7 %copy-start.1 = (bf16[1,128,5120]{2,1,0:T(8,128)(2,1)S(1)}, bf16[1,128,5120]{2,1,0:T(8,128)(2,1)}, u32[]{:S(2)}) copy-start(bf16[1,128,5120]{2,1,0:T(8,128)(2,1)} %param.17) | copy-start | bytes 3932164
  56.1 3.8 %collective-permute-start.2 = (bf16[32,56,128]{2,1,0:T(8,128)(2,1)S(1)}, bf16[32,56,128]{2,1,0:T(8,128)(2,1)S(1)}, u32[]{:S(2)}, u32[]{:S(2)}) collective-permute-start(bf16[32,56,128]{2,1,0:T(8,128)(2,1)S(1)} %get-tuple-element.27), channel_id=1, source_target_pairs={{0,1},{1,0},{2,3},{3,2},{4,5},{5,4},{6,7},{7,6},{8,9},{9,8},{10,11... | collective-permute-start | bytes 1376264 | tf_op jit(solution)/shard_map/ppermute | solution.py:266

commit v4 on v3

--- a/solution.py
+++ b/solution.py
@@ -17,6 +17,14 @@
 
 def onto(shape, dim):
     return lax.broadcasted_iota(jnp.int32, shape, dim)
+
+
+def parity(video, member, dp, seq):
+    return (member + 2 * member // seq + 2 * video // dp) % 2
+
+
+def own_parity():
+    return parity(lax.axis_index("dp"), lax.axis_index("seq"), lax.axis_size("dp"), lax.axis_size("seq"))
 
 
 def nt(a, b):
@@ -104,7 +112,7 @@
     ranks, cut = half.shape
     width = act.shape[1]
     each, quarter = ranks // 2, ranks // 8
-    c, hi = lax.axis_index("seq") % 2, lax.axis_index("dp") % 2
+    c, hi = own_parity(), lax.axis_index("dp") % 2
     part = (lax.axis_index("seq") + lax.axis_index("dp") // 2) % 2
 
     @pl.when(part == 0)
@@ -167,7 +175,7 @@
         acc = acc + blocks[i].astype(F32)
     total[...] = jnp.zeros_like(total)
     total[0:rows, :] = acc
-    q = lax.axis_index("seq") % 4
+    q = lax.axis_index("seq") // 2 % 2 * 2 + own_parity()
     quarter = ranks // 4
     shape = (8 * length, total.shape[0])
     r, k = onto(shape, 0), onto(shape, 1)
@@ -187,8 +195,9 @@
 def finish_kernel(parts, down, up, gain, tokens):
     heads = parts.shape[0]
     factor = tokens / parts[0, 7:8, 0:1]
+    flip = 2 * lax.axis_index("dp") // lax.axis_size("dp")
     for s in range(heads):
-        b = parts[s] * factor
+        b = parts[s // 2 * 2 + (s + 2 * s // heads + flip) % 2] * factor
         up[:, s * HD : (s + 1) * HD] = b[0:2]
         down[:, s * HD : (s + 1) * HD] = b[2:4]
         gain[:, s * HD : (s + 1) * HD] = b[6:7]
@@ -266,10 +275,12 @@
     partner = lax.ppermute(theirs, "seq", [(s, s ^ 1) for s in range(seq)])
     both = (mine + partner.astype(F32)).astype(BF16)
     length = dp // 2
+    at = [[[0, 0] for _ in range(seq // 2)] for _ in range(dp)]
+    for d in range(dp):
+        for m in range(seq):
+            at[d][m // 2][parity(d, m, dp, seq)] = d * seq + m
     planes = [
-        [(2 * z + x) * seq + 2 * i + c for x in range(2) for i in range(seq // 2)]
-        for z in range(length)
-        for c in range(2)
+        [at[2 * z + x][i][c] for x in range(2) for i in range(seq // 2)] for z in range(length) for c in range(2)
     ]
     blocks = lax.all_to_all(both, ("dp", "seq"), 0, 0, tiled=True, axis_index_groups=planes)
     rank_rows = pl.pallas_call(
@@ -280,8 +291,11 @@
         compiler_params=within(4),
         scratch_shapes=[pltpu.VMEM((128, HD), F32)],
     )(blocks)
-    along_z = [list(range(hi, dp, 2)) for hi in range(2)]
-    shares = lax.all_to_all(rank_rows.reshape(length, 8, HD), "dp", 0, 0, tiled=True, axis_index_groups=along_z)
+    along_z = [
+        [at[2 * z + hi][i][c] for z in range(length)] for hi in range(2) for i in range(seq // 2) for c in range(2)
+    ]
+    shares = rank_rows.reshape(length, 8, HD)
+    shares = lax.all_to_all(shares, ("dp", "seq"), 0, 0, tiled=True, axis_index_groups=along_z)
     share = jnp.sum(shares, axis=0)
     parts = lax.all_to_all(jnp.broadcast_to(share, (seq, 8, HD)), "seq", 0, 0, tiled=True)
     down, up, gain = pl.pallas_call(

time: 117 us -> 116 us (level)
  blocking collectives: 83.8 us -> 82.6 us
    all_to_all x1, blocking collectives: 16.1 us -> 13.2 us  [shards(): lax.all_to_all(jnp.broadcast_to(share, (seq, 8, HD)), 'seq', 0, 0, tiled=...]
    all_to_all x1, blocking collectives: 26.4 us -> 28.2 us  [shards(): lax.all_to_all(both, ('dp', 'seq'), 0, 0, tiled=True, axis_index_groups=p...]
where the time goes in v4:
time: 116 us; the launch traced here: 115 us
  blocking collectives  82.6 us (71%)
  starting transfers between devices  20.4 us (18%)
  waiting for transfers between devices  5.41 us (5%)
  Pallas kernels  4.99 us (4%)
    all_gather x1, blocking collectives, gather_ranks(): lax.all_gather(pair, ('dp', 'seq'), axis=0, tiled=True, axis_index_groups...  28.5 us
    all_to_all x1, blocking collectives, shards(): lax.all_to_all(both, ('dp', 'seq'), 0, 0, tiled=True, axis_index_groups=p...  28.2 us
    all_to_all x1, starting transfers between devices, shards(): tg = lax.all_to_all(tg, 'seq', 0, 0, tiled=True)  14.2 us
    all_to_all x1, blocking collectives, shards(): lax.all_to_all(jnp.broadcast_to(share, (seq, 8, HD)), 'seq', 0, 0, tiled=...  13.2 us
    all_to_all x1, blocking collectives, shards(): lax.all_to_all(shares, ('dp', 'seq'), 0, 0, tiled=True, axis_index_groups...  12.8 us
    ppermute x1, waiting for transfers between devices, gather_ranks(): near = lax.ppermute(own, 'dp', [(d, d ^ 1) for d in range(dp)])  3.92 us
    ppermute x1, starting transfers between devices, shards(): partner = lax.ppermute(theirs, 'seq', [(s, s ^ 1) for s in range(seq)])  2.4 us
  transfers between devices with their start and end apart: 4, of which 3 were waited for; matrix products, arithmetic and copies ran while one was open for 1% of the time, Pallas kernels for 2%

profile of v4, /device:TPU:1, one launch (start us, length us, event | category | flops | bytes accessed | tf_op | source)
XLA Modules:
  0.0 115.2 jit_solution(12490060288576770085)
XLA Ops:
  0.6 0.0 copy-start.7
  0.6 0.0 copy-start.8
  0.7 0.0 copy-start.9
  0.7 0.0 copy-start.10
  0.7 0.0 copy-start.5
  0.7 0.0 copy-start.4
  0.7 0.0 copy-start.6
  0.7 0.0 copy-start.3
  0.7 0.0 copy-start
  0.7 14.2 %all-to-all-start = ((bf16[32,128,128]{2,1,0:T(8,128)(2,1)}), bf16[32,128,128]{2,1,0:T(8,128)(2,1)S(1)}, u32[]{:S(2)}, u32[]{:S(2)}) async-start(bf16[32,128,128]{2,1,0:T(8,128)(2,1)} %bitcast.18), calls=%async_computation | async-start | bytes 2097152 | tf_op jit(solution)/shard_map/all_to_all | solution.py:243
  15.0 1.9 %collective-permute-start = (bf16[1,2,4608]{2,1,0:T(2,128)(2,1)S(1)}, bf16[1,2,4608]{2,1,0:T(2,128)(2,1)S(1)}, u32[]{:S(2)}, u32[]{:S(2)}) collective-permute-start(bf16[1,2,4608]{2,1,0:T(2,128)(2,1)S(1)} %broadcast_select_fusion), channel_id=1, source_target_pairs={{0,32},{32,0},{64,96},{96,64},{128,160},{160,128},{192,224},{224,1... | collective-permute-start | bytes 55304 | tf_op jit(solution)/shard_map/ppermute | solution.py:221
  17.1 0.4 multiply_multiply_fusion
  17.4 0.0 copy-start.2
  17.4 0.4 shard_map.139
  17.9 3.9 %collective-permute-done = bf16[1,2,4608]{2,1,0:T(2,128)(2,1)S(1)} collective-permute-done((bf16[1,2,4608]{2,1,0:T(2,128)(2,1)S(1)}, bf16[1,2,4608]{2,1,0:T(2,128)(2,1)S(1)}, u32[]{:S(2)}, u32[]{:S(2)}) %collective-permute-start) | collective-permute-done | bytes 18464 | tf_op jit(solution)/shard_map/ppermute | solution.py:221
  21.8 0.1 pad_maximum_fusion
  21.9 28.5 %all_gather.3 = bf16[24,2,4608]{2,1,0:T(2,128)(2,1)S(1)} all-gather(bf16[2,2,4608]{2,1,0:T(2,128)(2,1)S(1)} %pad_maximum_fusion), channel_id=1, replica_groups={{0,65,128,193,256,321,384,449,512,577,640,705},{1,64,129,192,257,320,38..., dimensions={0}, use_global_device_ids=true | all-gather | bytes 479232 | tf_op jit(solution)/shard_map/all_gather | solution.py:230
  50.3 0.2 reshape.33.half
  50.5 1.9 %collective-permute-start.1 = (bf16[48,4608]{1,0:T(8,128)(2,1)S(1)}, bf16[48,4608]{1,0:T(8,128)(2,1)S(1)}, u32[]{:S(2)}, u32[]{:S(2)}) collective-permute-start(bf16[48,4608]{1,0:T(8,128)(2,1)S(1)} %reshape.33.half), channel_id=1, source_target_pairs={{0,1},{1,0},{2,3},{3,2},{4,5},{5,4},{6,7},{7,6},{8,9},{9,8},{10,11... | collective-permute-start | bytes 1327112 | tf_op jit(solution)/shard_map/ppermute | solution.py:232
  52.4 0.0 all-to-all-done.tg
  52.5 0.0 copy-start.1
  52.5 1.7 %shard_map.140 = (bf16[128,4096]{1,0:T(8,128)(2,1)S(1)}, f32[32,8,128]{2,1,0:T(8,128)S(1)}) custom-call(bf16[32,128,128]{2,1,0:T(8,128)(2,1)S(1)} %all-to-all-done.tg, bf16[128,4096]{1,0:T(8,128)(2,1)S(1)} %bitcast.15, f32[128,128]{1,0:T(8,128)S(1)} %get-tuple-element.21.cos, f32[128,128]{1,0:T(8,128)S(1)} %get-tuple-element.22.sin, ...), custom_call_target="tpu_custom_call" | custom-call | tf_op jit(solution)/shard_map/pallas_call | solution.py:253
  54.1 0.1 collective-permute-done.1.other
  54.2 1.9 %shard_map.141 = (f32[32,56,128]{2,1,0:T(8,128)S(1)}, bf16[32,56,128]{2,1,0:T(8,128)(2,1)S(1)}) custom-call(bf16[128,5120]{1,0:T(8,128)(2,1)S(1)} %bitcast.16, bf16[48,4608]{1,0:T(8,128)(2,1)S(1)} %reshape.33.half, bf16[48,4608]{1,0:T(8,128)(2,1)S(1)} %collective-permute-done.1.other, bf16[128,4096]{1,0:T(8,128)(2,1)S(1)} %get-tuple-element.24.delta, ...), custom_call_target="tpu_custom_call" | custom-call | tf_op jit(solution)/shard_map/pallas_call | solution.py:264
  56.1 2.4 %collective-permute-start.2 = (bf16[32,56,128]{2,1,0:T(8,128)(2,1)S(1)}, bf16[32,56,128]{2,1,0:T(8,128)(2,1)S(1)}, u32[]{:S(2)}, u32[]{:S(2)}) collective-permute-start(bf16[32,56,128]{2,1,0:T(8,128)(2,1)S(1)} %get-tuple-element.27), channel_id=1, source_target_pairs={{0,1},{1,0},{2,3},{3,2},{4,5},{5,4},{6,7},{7,6},{8,9},{9,8},{10,11... | collective-permute-start | bytes 1376264 | tf_op jit(solution)/shard_map/ppermute | solution.py:275
  58.5 1.4 %collective-permute-done.2 = bf16[32,56,128]{2,1,0:T(8,128)(2,1)S(1)} collective-permute-done((bf16[32,56,128]{2,1,0:T(8,128)(2,1)S(1)}, bf16[32,56,128]{2,1,0:T(8,128)(2,1)S(1)}, u32[]{:S(2)}, u32[]{:S(2)}) %collective-permute-start.2) | collective-permute-done | bytes 458784 | tf_op jit(solution)/shard_map/ppermute | solution.py:275
  59.9 0.1 add_convert_fusion
  60.0 28.2 %all_to_all.20.refs_0_ = bf16[32,56,128]{2,1,0:T(8,128)(2,1)S(1)} all-to-all(bf16[32,56,128]{2,1,0:T(8,128)(2,1)S(1)} %add_convert_fusion), channel_id=1, replica_groups={{0,2,4,6,8,10,12,14,17,19,21,23,25,27,29,31,32,34,36,38,40,42,44,46,49,..., dimensions={0} | all-to-all | bytes 917504 | tf_op jit(solution)/shard_map/all_to_all | solution.py:285
  88.2 0.3 shard_map.142
  88.4 12.8 %all_to_all.21 = f32[12,8,128]{2,1,0:T(8,128)S(1)} all-to-all(f32[12,8,128]{2,1,0:T(8,128)S(1)} %bitcast.17), channel_id=1, replica_groups={{0,64,128,192,256,320,385,449,513,577,641,705},{1,65,129,193,257,321,38..., dimensions={0} | all-to-all | bytes 98304 | tf_op jit(solution)/shard_map/all_to_all | solution.py:298
  101.2 13.2 %all_to_all.22.refs_0_ = f32[32,8,128]{2,1,0:T(8,128)S(1)} all-to-all(f32[32,8,128]{2,1,0:T(8,128)S(1)} %broadcast_in_dim.58), channel_id=1, replica_groups=mesh['dp'=24,'seq'=32] {'seq'}, dimensions={0} | all-to-all | bytes 262144 | tf_op jit(solution)/shard_map/all_to_all | solution.py:300
  114.4 0.8 shard_map.143
  (17 shorter events, 0.1 us)
Async XLA Ops:
  0.6 16.4 %copy-start.7 = (f32[128]{0:T(128)S(1)}, f32[128]{0:T(128)}, u32[]{:S(2)}) copy-start(f32[128]{0:T(128)} %constant.46.clone) | copy-start | bytes 1540
  0.6 16.4 %copy-start.8 = (f32[128]{0:T(128)S(1)}, f32[128]{0:T(128)}, u32[]{:S(2)}) copy-start(f32[128]{0:T(128)} %constant.45.clone) | copy-start | bytes 1540
  0.7 16.4 %copy-start.9 = (pred[128]{0:T(512)(128)(4,1)S(1)}, pred[128]{0:T(512)(128)(4,1)}, u32[]{:S(2)}) copy-start(pred[128]{0:T(512)(128)(4,1)} %constant.44.clone) | copy-start | bytes 388
  0.7 16.4 %copy-start.10 = (pred[128]{0:T(512)(128)(4,1)S(1)}, pred[128]{0:T(512)(128)(4,1)}, u32[]{:S(2)}) copy-start(pred[128]{0:T(512)(128)(4,1)} %constant.43.clone) | copy-start | bytes 388
  0.7 14.3 %copy-start.5 = (bf16[1,2,4096]{2,1,0:T(2,128)(2,1)S(1)}, bf16[1,2,4096]{2,1,0:T(2,128)(2,1)}, u32[]{:S(2)}) copy-start(bf16[1,2,4096]{2,1,0:T(2,128)(2,1)} %param.16) | copy-start | bytes 49156
  0.7 14.3 %copy-start.4 = (bf16[1,2,5120]{2,1,0:T(2,128)(2,1)S(1)}, bf16[1,2,5120]{2,1,0:T(2,128)(2,1)}, u32[]{:S(2)}) copy-start(bf16[1,2,5120]{2,1,0:T(2,128)(2,1)} %param.15) | copy-start | bytes 61444
  0.7 16.3 %copy-start.6 = (s32[3,1,128]{2,1,0:T(1,128)S(1)}, s32[3,1,128]{2,1,0:T(1,128)}, u32[]{:S(2)}) copy-start(s32[3,1,128]{2,1,0:T(1,128)} %param.18) | copy-start | bytes 4612
  0.7 16.3 %copy-start.3 = (s32[1,128]{1,0:T(1,128)S(1)}, s32[1,128]{1,0:T(1,128)}, u32[]{:S(2)}) copy-start(s32[1,128]{1,0:T(1,128)} %valid.1) | copy-start | bytes 1540
  0.7 16.7 %copy-start = (bf16[1,1,128,4096]{3,2,1,0:T(8,128)(2,1)S(1)}, bf16[1,1,128,4096]{3,2,1,0:T(8,128)(2,1)}, u32[]{:S(2)}) copy-start(bf16[1,1,128,4096]{3,2,1,0:T(8,128)(2,1)} %param.12) | copy-start | bytes 3145732
  0.7 51.7 %all-to-all-start = ((bf16[32,128,128]{2,1,0:T(8,128)(2,1)}), bf16[32,128,128]{2,1,0:T(8,128)(2,1)S(1)}, u32[]{:S(2)}, u32[]{:S(2)}) async-start(bf16[32,128,128]{2,1,0:T(8,128)(2,1)} %bitcast.18), calls=%async_computation | async-start | bytes 2097152 | tf_op jit(solution)/shard_map/all_to_all | solution.py:243
  15.0 6.8 %collective-permute-start = (bf16[1,2,4608]{2,1,0:T(2,128)(2,1)S(1)}, bf16[1,2,4608]{2,1,0:T(2,128)(2,1)S(1)}, u32[]{:S(2)}, u32[]{:S(2)}) collective-permute-start(bf16[1,2,4608]{2,1,0:T(2,128)(2,1)S(1)} %broadcast_select_fusion), channel_id=1, source_target_pairs={{0,32},{32,0},{64,96},{96,64},{128,160},{160,128},{192,224},{224,1... | collective-permute-start | bytes 55304 | tf_op jit(solution)/shard_map/ppermute | solution.py:221
  17.4 35.0 %copy-start.2 = (f32[1,4096]{1,0:T(1,128)S(1)}, f32[1,4096]{1,0:T(1,128)}, u32[]{:S(2)}) copy-start(f32[1,4096]{1,0:T(1,128)} %gains.1) | copy-start | bytes 49156
  50.5 3.7 %collective-permute-start.1 = (bf16[48,4608]{1,0:T(8,128)(2,1)S(1)}, bf16[48,4608]{1,0:T(8,128)(2,1)S(1)}, u32[]{:S(2)}, u32[]{:S(2)}) collective-permute-start(bf16[48,4608]{1,0:T(8,128)(2,1)S(1)} %reshape.33.half), channel_id=1, source_target_pairs={{0,1},{1,0},{2,3},{3,2},{4,5},{5,4},{6,7},{7,6},{8,9},{9,8},{10,11... | collective-permute-start | bytes 1327112 | tf_op jit(solution)/shard_map/ppermute | solution.py:232
  52.5 1.7 %copy-start.1 = (bf16[1,128,5120]{2,1,0:T(8,128)(2,1)S(1)}, bf16[1,128,5120]{2,1,0:T(8,128)(2,1)}, u32[]{:S(2)}) copy-start(bf16[1,128,5120]{2,1,0:T(8,128)(2,1)} %param.17) | copy-start | bytes 3932164
  56.1 3.8 %collective-permute-start.2 = (bf16[32,56,128]{2,1,0:T(8,128)(2,1)S(1)}, bf16[32,56,128]{2,1,0:T(8,128)(2,1)S(1)}, u32[]{:S(2)}, u32[]{:S(2)}) collective-permute-start(bf16[32,56,128]{2,1,0:T(8,128)(2,1)S(1)} %get-tuple-element.27), channel_id=1, source_target_pairs={{0,1},{1,0},{2,3},{3,2},{4,5},{5,4},{6,7},{7,6},{8,9},{9,8},{10,11... | collective-permute-start | bytes 1376264 | tf_op jit(solution)/shard_map/ppermute | solution.py:275

commit v5 on v4

--- a/solution.py
+++ b/solution.py
@@ -113,7 +113,7 @@
     width = act.shape[1]
     each, quarter = ranks // 2, ranks // 8
     c, hi = own_parity(), lax.axis_index("dp") % 2
-    part = (lax.axis_index("seq") + lax.axis_index("dp") // 2) % 2
+    part = (lax.axis_index("seq") + lax.axis_index("dp") // 2 + lax.axis_index("dp")) % 2
 
     @pl.when(part == 0)
     def _():
@@ -160,12 +160,12 @@
                     pieces.append((ups[rows, cols], downs[rows, cols], rest))
                 for j, (top, size) in enumerate(((0, each), (each, each), (2 * each, REM))):
                     even, odd = pieces[0][j], pieces[1][j]
-                    at = x * (heads // 2) + i
+                    at = 2 * i + x
                     mine[at, top : top + size, :] = jnp.where(c == 0, even, odd)
                     theirs[at, top : top + size, :] = jnp.where(c == 0, odd, even).astype(theirs.dtype)
         return 0
 
-    lax.fori_loop(0, heads // 4, four, 0, unroll=4)
+    lax.fori_loop(0, heads // 4, four, 0, unroll=8)
 
 
 def spread_kernel(blocks, out, total, ranks, length):
@@ -216,9 +216,11 @@
 def gather_ranks(adapter_lowering, adapter_raising, dp, seq, member, small):
     own = jnp.concatenate([adapter_lowering, adapter_raising], axis=2)
     cut = own.shape[2] // 2
-    part = (member + lax.axis_index("dp") // 2) % 2
+    video = lax.axis_index("dp")
+    part = (member + video // 2 + video) % 2
     own = jnp.where(part == 0, own[:, :, :cut], own[:, :, cut:])
-    near = lax.ppermute(own, "dp", [(d, d ^ 1) for d in range(dp)])
+    moves = [(d * seq + m, (d ^ 1) * seq + (m ^ 1)) for d in range(dp) for m in range(seq)]
+    near = lax.ppermute(own, ("dp", "seq"), moves)
     pair = jnp.concatenate([own, near], axis=0)
     pair, small = lax.optimization_barrier((pair, small))
     rings = [
@@ -280,7 +282,7 @@
         for m in range(seq):
             at[d][m // 2][parity(d, m, dp, seq)] = d * seq + m
     planes = [
-        [at[2 * z + x][i][c] for x in range(2) for i in range(seq // 2)] for z in range(length) for c in range(2)
+        [at[2 * z + x][i][c] for i in range(seq // 2) for x in range(2)] for z in range(length) for c in range(2)
     ]
     blocks = lax.all_to_all(both, ("dp", "seq"), 0, 0, tiled=True, axis_index_groups=planes)
     rank_rows = pl.pallas_call(

time: 116 us -> 115 us (level)
  blocking collectives: 82.6 us -> 81.3 us
    all_to_all x1, blocking collectives: 28.2 us -> 26.1 us  [shards(): lax.all_to_all(both, ('dp', 'seq'), 0, 0, tiled=True, axis_index_groups=p...]
  transfers between devices with their start and end apart: 4 -> 4, of which waited for: 3 -> 2; matrix products, arithmetic and copies ran while one was open for 1% -> 1% of each run, Pallas kernels for 2% -> 2%
where the time goes in v5:
time: 115 us
  blocking collectives  81.3 us (71%)
  starting transfers between devices  20.6 us (18%)
  waiting for transfers between devices  6.2 us (5%)
  Pallas kernels  4.92 us (4%)
    all_gather x1, blocking collectives, gather_ranks(): lax.all_gather(pair, ('dp', 'seq'), axis=0, tiled=True, axis_index_groups...  28.1 us
    all_to_all x1, blocking collectives, shards(): lax.all_to_all(both, ('dp', 'seq'), 0, 0, tiled=True, axis_index_groups=p...  26.1 us
    all_to_all x1, starting transfers between devices, shards(): tg = lax.all_to_all(tg, 'seq', 0, 0, tiled=True)  14.2 us
    all_to_all x1, blocking collectives, shards(): lax.all_to_all(jnp.broadcast_to(share, (seq, 8, HD)), 'seq', 0, 0, tiled=...  14 us
    all_to_all x1, blocking collectives, shards(): lax.all_to_all(shares, ('dp', 'seq'), 0, 0, tiled=True, axis_index_groups...  13.1 us
    ppermute x1, waiting for transfers between devices, gather_ranks(): near = lax.ppermute(own, ('dp', 'seq'), moves)  4.42 us
    ppermute x1, starting transfers between devices, gather_ranks(): other = lax.ppermute(half, 'seq', [(s, s ^ 1) for s in range(seq)])  2.57 us
  transfers between devices with their start and end apart: 4, of which 2 were waited for; matrix products, arithmetic and copies ran while one was open for 1% of the time, Pallas kernels for 2%

profile of v5, /device:TPU:1, one launch (start us, length us, event | category | flops | bytes accessed | tf_op | source)
XLA Modules:
  0.0 114.8 jit_solution(5995719218051339663)
XLA Ops:
  0.6 0.0 copy-start.7
  0.6 0.0 copy-start.8
  0.7 0.0 copy-start.9
  0.7 0.0 copy-start.10
  0.7 0.0 copy-start.5
  0.7 0.0 copy-start.4
  0.7 14.2 %all-to-all-start = ((bf16[32,128,128]{2,1,0:T(8,128)(2,1)}), bf16[32,128,128]{2,1,0:T(8,128)(2,1)S(1)}, u32[]{:S(2)}, u32[]{:S(2)}) async-start(bf16[32,128,128]{2,1,0:T(8,128)(2,1)} %bitcast.18), calls=%async_computation | async-start | bytes 2097152 | tf_op jit(solution)/shard_map/all_to_all | solution.py:245
  15.0 1.9 %collective-permute-start = (bf16[1,2,4608]{2,1,0:T(2,128)(2,1)S(1)}, bf16[1,2,4608]{2,1,0:T(2,128)(2,1)S(1)}, u32[]{:S(2)}, u32[]{:S(2)}) collective-permute-start(bf16[1,2,4608]{2,1,0:T(2,128)(2,1)S(1)} %broadcast_select_fusion), channel_id=1, source_target_pairs={{0,33},{1,32},{2,35},{3,34},{4,37},{5,36},{6,39},{7,38},{8,41},{9,... | collective-permute-start | bytes 55304 | tf_op jit(solution)/shard_map/ppermute | solution.py:223
  17.0 0.0 copy-done.3
  17.1 0.4 multiply_multiply_fusion
  17.4 0.0 copy-done
  17.4 0.0 copy-start.2
  17.4 0.4 shard_map.139
  17.9 4.4 %collective-permute-done = bf16[1,2,4608]{2,1,0:T(2,128)(2,1)S(1)} collective-permute-done((bf16[1,2,4608]{2,1,0:T(2,128)(2,1)S(1)}, bf16[1,2,4608]{2,1,0:T(2,128)(2,1)S(1)}, u32[]{:S(2)}, u32[]{:S(2)}) %collective-permute-start) | collective-permute-done | bytes 18464 | tf_op jit(solution)/shard_map/ppermute | solution.py:223
  22.3 0.1 pad_maximum_fusion
  22.4 28.1 %all_gather.3 = bf16[24,2,4608]{2,1,0:T(2,128)(2,1)S(1)} all-gather(bf16[2,2,4608]{2,1,0:T(2,128)(2,1)S(1)} %pad_maximum_fusion), channel_id=1, replica_groups={{0,65,128,193,256,321,384,449,512,577,640,705},{1,64,129,192,257,320,38..., dimensions={0}, use_global_device_ids=true | all-gather | bytes 479232 | tf_op jit(solution)/shard_map/all_gather | solution.py:232
  50.4 0.2 reshape.33.half
  50.6 2.6 %collective-permute-start.1 = (bf16[48,4608]{1,0:T(8,128)(2,1)S(1)}, bf16[48,4608]{1,0:T(8,128)(2,1)S(1)}, u32[]{:S(2)}, u32[]{:S(2)}) collective-permute-start(bf16[48,4608]{1,0:T(8,128)(2,1)S(1)} %reshape.33.half), channel_id=1, source_target_pairs={{0,1},{1,0},{2,3},{3,2},{4,5},{5,4},{6,7},{7,6},{8,9},{9,8},{10,11... | collective-permute-start | bytes 1327112 | tf_op jit(solution)/shard_map/ppermute | solution.py:234
  53.2 0.0 all-to-all-done.tg
  53.2 0.0 copy-start.1
  53.2 1.7 %shard_map.140 = (bf16[128,4096]{1,0:T(8,128)(2,1)S(1)}, f32[32,8,128]{2,1,0:T(8,128)S(1)}) custom-call(bf16[32,128,128]{2,1,0:T(8,128)(2,1)S(1)} %all-to-all-done.tg, bf16[128,4096]{1,0:T(8,128)(2,1)S(1)} %bitcast.15, f32[128,128]{1,0:T(8,128)S(1)} %get-tuple-element.21.cos, f32[128,128]{1,0:T(8,128)S(1)} %get-tuple-element.22.sin, ...), custom_call_target="tpu_custom_call" | custom-call | tf_op jit(solution)/shard_map/pallas_call | solution.py:255
  54.9 0.0 collective-permute-done.1.other
  54.9 0.0 copy-done.1
  54.9 1.8 %shard_map.141 = (f32[32,56,128]{2,1,0:T(8,128)S(1)}, bf16[32,56,128]{2,1,0:T(8,128)(2,1)S(1)}) custom-call(bf16[128,5120]{1,0:T(8,128)(2,1)S(1)} %bitcast.16, bf16[48,4608]{1,0:T(8,128)(2,1)S(1)} %reshape.33.half, bf16[48,4608]{1,0:T(8,128)(2,1)S(1)} %collective-permute-done.1.other, bf16[128,4096]{1,0:T(8,128)(2,1)S(1)} %get-tuple-element.24.delta, ...), custom_call_target="tpu_custom_call" | custom-call | tf_op jit(solution)/shard_map/pallas_call | solution.py:266
  56.7 1.9 %collective-permute-start.2 = (bf16[32,56,128]{2,1,0:T(8,128)(2,1)S(1)}, bf16[32,56,128]{2,1,0:T(8,128)(2,1)S(1)}, u32[]{:S(2)}, u32[]{:S(2)}) collective-permute-start(bf16[32,56,128]{2,1,0:T(8,128)(2,1)S(1)} %get-tuple-element.27), channel_id=1, source_target_pairs={{0,1},{1,0},{2,3},{3,2},{4,5},{5,4},{6,7},{7,6},{8,9},{9,8},{10,11... | collective-permute-start | bytes 1376264 | tf_op jit(solution)/shard_map/ppermute | solution.py:277
  58.6 1.8 %collective-permute-done.2 = bf16[32,56,128]{2,1,0:T(8,128)(2,1)S(1)} collective-permute-done((bf16[32,56,128]{2,1,0:T(8,128)(2,1)S(1)}, bf16[32,56,128]{2,1,0:T(8,128)(2,1)S(1)}, u32[]{:S(2)}, u32[]{:S(2)}) %collective-permute-start.2) | collective-permute-done | bytes 458784 | tf_op jit(solution)/shard_map/ppermute | solution.py:277
  60.4 0.1 add_convert_fusion
  60.5 26.1 %all_to_all.20.refs_0_ = bf16[32,56,128]{2,1,0:T(8,128)(2,1)S(1)} all-to-all(bf16[32,56,128]{2,1,0:T(8,128)(2,1)S(1)} %add_convert_fusion), channel_id=1, replica_groups={{0,32,2,34,4,36,6,38,8,40,10,42,12,44,14,46,17,49,19,51,21,53,23,55,25,..., dimensions={0} | all-to-all | bytes 917504 | tf_op jit(solution)/shard_map/all_to_all | solution.py:287
  86.6 0.3 shard_map.142
  86.9 13.1 %all_to_all.21 = f32[12,8,128]{2,1,0:T(8,128)S(1)} all-to-all(f32[12,8,128]{2,1,0:T(8,128)S(1)} %bitcast.17), channel_id=1, replica_groups={{0,64,128,192,256,320,385,449,513,577,641,705},{1,65,129,193,257,321,38..., dimensions={0} | all-to-all | bytes 98304 | tf_op jit(solution)/shard_map/all_to_all | solution.py:300
  100.0 14.0 %all_to_all.22.refs_0_ = f32[32,8,128]{2,1,0:T(8,128)S(1)} all-to-all(f32[32,8,128]{2,1,0:T(8,128)S(1)} %broadcast_in_dim.58), channel_id=1, replica_groups=mesh['dp'=24,'seq'=32] {'seq'}, dimensions={0} | all-to-all | bytes 262144 | tf_op jit(solution)/shard_map/all_to_all | solution.py:302
  114.0 0.8 shard_map.143
  (17 shorter events, 0.1 us)
Async XLA Ops:
  0.6 16.4 %copy-start.7 = (f32[128]{0:T(128)S(1)}, f32[128]{0:T(128)}, u32[]{:S(2)}) copy-start(f32[128]{0:T(128)} %constant.46.clone) | copy-start | bytes 1540
  0.6 16.4 %copy-start.8 = (f32[128]{0:T(128)S(1)}, f32[128]{0:T(128)}, u32[]{:S(2)}) copy-start(f32[128]{0:T(128)} %constant.45.clone) | copy-start | bytes 1540
  0.7 16.4 %copy-start.9 = (pred[128]{0:T(512)(128)(4,1)S(1)}, pred[128]{0:T(512)(128)(4,1)}, u32[]{:S(2)}) copy-start(pred[128]{0:T(512)(128)(4,1)} %constant.44.clone) | copy-start | bytes 388
  0.7 16.4 %copy-start.10 = (pred[128]{0:T(512)(128)(4,1)S(1)}, pred[128]{0:T(512)(128)(4,1)}, u32[]{:S(2)}) copy-start(pred[128]{0:T(512)(128)(4,1)} %constant.43.clone) | copy-start | bytes 388
  0.7 14.3 %copy-start.5 = (bf16[1,2,4096]{2,1,0:T(2,128)(2,1)S(1)}, bf16[1,2,4096]{2,1,0:T(2,128)(2,1)}, u32[]{:S(2)}) copy-start(bf16[1,2,4096]{2,1,0:T(2,128)(2,1)} %param.16) | copy-start | bytes 49156
  0.7 14.3 %copy-start.4 = (bf16[1,2,5120]{2,1,0:T(2,128)(2,1)S(1)}, bf16[1,2,5120]{2,1,0:T(2,128)(2,1)}, u32[]{:S(2)}) copy-start(bf16[1,2,5120]{2,1,0:T(2,128)(2,1)} %param.15) | copy-start | bytes 61444
  0.7 16.3 %copy-start.6 = (s32[3,1,128]{2,1,0:T(1,128)S(1)}, s32[3,1,128]{2,1,0:T(1,128)}, u32[]{:S(2)}) copy-start(s32[3,1,128]{2,1,0:T(1,128)} %param.18) | copy-start | bytes 4612
  0.7 16.3 %copy-start.3 = (s32[1,128]{1,0:T(1,128)S(1)}, s32[1,128]{1,0:T(1,128)}, u32[]{:S(2)}) copy-start(s32[1,128]{1,0:T(1,128)} %valid.1) | copy-start | bytes 1540
  0.7 16.7 %copy-start = (bf16[1,1,128,4096]{3,2,1,0:T(8,128)(2,1)S(1)}, bf16[1,1,128,4096]{3,2,1,0:T(8,128)(2,1)}, u32[]{:S(2)}) copy-start(bf16[1,1,128,4096]{3,2,1,0:T(8,128)(2,1)} %param.12) | copy-start | bytes 3145732
  0.7 52.5 %all-to-all-start = ((bf16[32,128,128]{2,1,0:T(8,128)(2,1)}), bf16[32,128,128]{2,1,0:T(8,128)(2,1)S(1)}, u32[]{:S(2)}, u32[]{:S(2)}) async-start(bf16[32,128,128]{2,1,0:T(8,128)(2,1)} %bitcast.18), calls=%async_computation | async-start | bytes 2097152 | tf_op jit(solution)/shard_map/all_to_all | solution.py:245
  15.0 7.3 %collective-permute-start = (bf16[1,2,4608]{2,1,0:T(2,128)(2,1)S(1)}, bf16[1,2,4608]{2,1,0:T(2,128)(2,1)S(1)}, u32[]{:S(2)}, u32[]{:S(2)}) collective-permute-start(bf16[1,2,4608]{2,1,0:T(2,128)(2,1)S(1)} %broadcast_select_fusion), channel_id=1, source_target_pairs={{0,33},{1,32},{2,35},{3,34},{4,37},{5,36},{6,39},{7,38},{8,41},{9,... | collective-permute-start | bytes 55304 | tf_op jit(solution)/shard_map/ppermute | solution.py:223
  17.4 35.8 %copy-start.2 = (f32[1,4096]{1,0:T(1,128)S(1)}, f32[1,4096]{1,0:T(1,128)}, u32[]{:S(2)}) copy-start(f32[1,4096]{1,0:T(1,128)} %gains.1) | copy-start | bytes 49156
  50.6 4.3 %collective-permute-start.1 = (bf16[48,4608]{1,0:T(8,128)(2,1)S(1)}, bf16[48,4608]{1,0:T(8,128)(2,1)S(1)}, u32[]{:S(2)}, u32[]{:S(2)}) collective-permute-start(bf16[48,4608]{1,0:T(8,128)(2,1)S(1)} %reshape.33.half), channel_id=1, source_target_pairs={{0,1},{1,0},{2,3},{3,2},{4,5},{5,4},{6,7},{7,6},{8,9},{9,8},{10,11... | collective-permute-start | bytes 1327112 | tf_op jit(solution)/shard_map/ppermute | solution.py:234
  53.2 1.7 %copy-start.1 = (bf16[1,128,5120]{2,1,0:T(8,128)(2,1)S(1)}, bf16[1,128,5120]{2,1,0:T(8,128)(2,1)}, u32[]{:S(2)}) copy-start(bf16[1,128,5120]{2,1,0:T(8,128)(2,1)} %param.17) | copy-start | bytes 3932164
  56.7 3.7 %collective-permute-start.2 = (bf16[32,56,128]{2,1,0:T(8,128)(2,1)S(1)}, bf16[32,56,128]{2,1,0:T(8,128)(2,1)S(1)}, u32[]{:S(2)}, u32[]{:S(2)}) collective-permute-start(bf16[32,56,128]{2,1,0:T(8,128)(2,1)S(1)} %get-tuple-element.27), channel_id=1, source_target_pairs={{0,1},{1,0},{2,3},{3,2},{4,5},{5,4},{6,7},{7,6},{8,9},{9,8},{10,11... | collective-permute-start | bytes 1376264 | tf_op jit(solution)/shard_map/ppermute | solution.py:277
